TPU v7x, 128 devices: a whole 4x4x4 slice. The times are simulated.
128 devices in a mesh: gx: 4 (over y), gz: 32 (over x, z, core).
Axes of the slice: x: 4, y: 4, z: 4, core: 2. Of those that a mesh axis runs over, the one named last changes fastest.
Arguments:
- divergence: float32 [256, 512, 512], P('gx', 'gz'), may hold values from -18 to 18
- level_set: float32 [256, 512, 512], P('gx', 'gz'), may hold values from -2 to 2, as said below
- tile_ids: int32 [4, 32768], P('gx', 'gz'), may hold values from -1 to 1023, as said below
Outputs:
- pressure: float32 [256, 512, 512], P('gx', 'gz')
- residual: float32 [256, 512, 512], P('gx', 'gz')
Inputs may be any that keep to these rules, and one draw needn't show every extreme that they name: `level_set`: every entry lies at least 0.05 away from zero. `tile_ids`: each device's part lists distinct tile numbers of its own block, below 1024, in increasing order, followed by -1 entries; some device lists all 1024 and some device lists none.
All inputs are finite; a program needn't handle non-finite values.
Results may differ from a plain program's by a relative error of at most 0.0003.
Values sent between devices are 32-bit elements; how exact they have to be, the bound alone decides.
A program may use at most 128 MiB of HBM per device.

v0:
```python
import functools

import jax
import jax.numpy as jnp
from jax import lax
from jax.sharding import Mesh
from jax.sharding import PartitionSpec as P

ITERS = 2
TILE = 8
GX_GZ = ("gx", "gz_0", "gz_1", "gz_2")
GZ = ("gz_0", "gz_1", "gz_2")


damping = 2.0 / 3.0
ratio_cap = 20.0


def with_halo(array, sides, width):
    edges = {}
    for axis, dim in sides:
        peers, length = (lax.axis_size(axis), array.shape[dim])
        up = [(i, (i + 1) % peers) for i in range(peers - 1)]
        last = lax.slice_in_dim(array, length - width, length, axis=dim)
        leading = lax.slice_in_dim(array, 0, width, axis=dim)
        edges[dim] = (
            lax.ppermute(last, axis, up),
            lax.ppermute(leading, axis, [(b, a) for a, b in up]),
        )
    done = []
    for _, dim in sides:
        low, high = edges[dim]
        around = [(width, width) if d in done else (0, 0) for d in range(array.ndim)]
        array = jnp.concatenate([jnp.pad(low, around), array, jnp.pad(high, around)], axis=dim)
        done.append(dim)
    return array


def by_axis(array, axes):
    return functools.reduce(lax.psum, axes, array)


def beside(values):
    center = values[1:-1, 1:-1]
    upward = jnp.concatenate([center[:, :, 1:], jnp.zeros_like(center[:, :, :1])], 2)
    downward = jnp.concatenate([jnp.zeros_like(center[:, :, :1]), center[:, :, :-1]], 2)
    return [
        values[2:, 1:-1],
        values[:-2, 1:-1],
        values[1:-1, 2:],
        values[1:-1, :-2],
        upward,
        downward,
    ]


def beside_all(values):
    pieces = beside(values)
    result = pieces[0] + pieces[1]
    for addend in pieces[2:]:
        result = result + addend
    return result


def coefficients(dist_ext, fluid_ext):
    dist_mid = dist_ext[1:-1, 1:-1]
    fluid_mid = fluid_ext[1:-1, 1:-1]
    safe_dist = jnp.where(dist_mid > 0, dist_mid, 1.0)
    term_list = [
        jnp.where(fluid_side > 0, 1.0, jnp.minimum((dist_mid + dist_side) / safe_dist, ratio_cap))
        for dist_side, fluid_side in zip(beside(dist_ext), beside(fluid_ext))
    ]
    result = term_list[0] + term_list[1]
    for addend in term_list[2:]:
        result = result + addend
    return (jnp.where(fluid_mid > 0, result, 1.0), fluid_mid)


def on_device(divergence, level_set, tile_ids):
    size_x, size_z, size_y = divergence.shape
    tiles_x, tiles_z, tiles_y = (size_x // TILE, size_z // TILE, size_y // TILE)
    listed = tile_ids.reshape(-1)
    numbers = lax.broadcasted_iota(jnp.int32, (1, tiles_x * tiles_z * tiles_y), 1)
    listed_hit = (
        jnp.any(listed[:, None] == numbers, axis=0)
        .astype(jnp.float32)
        .reshape(tiles_x, tiles_z, tiles_y)
    )
    active = jnp.broadcast_to(
        listed_hit[:, None, :, None, :, None], (tiles_x, TILE, tiles_z, TILE, tiles_y, TILE)
    ).reshape(size_x, size_z, size_y)
    fluid_cells = jnp.where(level_set < 0, active, 0.0)
    distance = jnp.abs(level_set)
    stacked = jnp.stack((distance, fluid_cells))
    near_cells = with_halo(stacked, (("gx", 1), (GZ, 2)), 1)
    diag_mid, fluid_mid = coefficients(near_cells[0], near_cells[1])
    scale_mid = damping / diag_mid

    def operate(values):
        padded = with_halo(values, (("gx", 0), (GZ, 1)), 1)
        return fluid_mid * (diag_mid * values - beside_all(padded))

    def precondition(residual):
        first_pass = scale_mid * residual
        second_pass = first_pass + scale_mid * (residual - operate(first_pass))
        return (second_pass, operate(second_pass))

    pressure = jnp.zeros_like(divergence)
    residual = fluid_mid * divergence
    smoothed, precond_image = precondition(residual)
    direction = smoothed
    operated = precond_image

    def both_sums(current, preconditioned, image_of):
        return (
            by_axis(jnp.sum(current * preconditioned), GX_GZ),
            by_axis(jnp.sum(image_of * preconditioned), GX_GZ),
        )

    gamma_now, delta_now = both_sums(residual, smoothed, precond_image)
    alpha_now = gamma_now / delta_now
    for iteration in range(ITERS):
        pressure = pressure + alpha_now * direction
        residual = residual - alpha_now * operated
        if iteration + 1 < ITERS:
            smoothed, precond_image = precondition(residual)
            gamma_next, delta_now = both_sums(residual, smoothed, precond_image)
            beta_now = gamma_next / gamma_now
            alpha_now = gamma_next / (delta_now - beta_now * gamma_next / alpha_now)
            direction = smoothed + beta_now * direction
            operated = precond_image + beta_now * operated
            gamma_now = gamma_next
    return (pressure, residual)


def solution(mesh):
    torus = Mesh(mesh.devices.reshape(mesh.shape["gx"], 4, 4, 2), ("gx", "gz_0", "gz_1", "gz_2"))
    in_specs = (P("gx", GZ, None), P("gx", GZ, None), P("gx", GZ))
    out_specs = (P("gx", GZ, None), P("gx", GZ, None))
    return jax.shard_map(
        on_device, mesh=torus, in_specs=in_specs, out_specs=out_specs, check_vma=False
    )
```

profile of v0, /device:TPU:1, one launch (start us, length us, event | category | flops | bytes accessed | tf_op | source)
XLA Modules:
  0.0 244.9 jit_solution(12363223627569875023)
XLA Ops:
  2.0 11.3 %broadcast_in_dim.18 = f32[8,8,2,8,64,8]{5,4,3,2,1,0:T(8,128)} broadcast(f32[8,2,64]{2,1,0:T(2,128)S(1)} %reshape.16), dimensions={0,2,4} | broadcast | bytes 2101248 | tf_op jit(solution)/shard_map/broadcast_in_dim | solution.py:89
  13.4 25.1 %reshape.15 = f32[64,16,512]{2,1,0:T(8,128)} reshape(f32[8,8,2,8,64,8]{5,4,3,2,1,0:T(8,128)} %broadcast_in_dim.18) | data formatting | bytes 4194304 | tf_op jit(solution)/shard_map/reshape | solution.py:91
  38.4 3.0 %abs_bitcast_fusion = (f32[1,64,16,512]{3,2,1,0:T(8,128)S(1)}, f32[1,64,16,512]{3,2,1,0:T(8,128)S(1)}) fusion(f32[64,16,512]{2,1,0:T(8,128)} %param.4, f32[64,16,512]{2,1,0:T(8,128)} %reshape.15), kind=kLoop, calls=%fused_computation.127 | loop fusion | flops 1572864 | bytes 8388608 | tf_op jit(solution)/shard_map/stack | solution.py:94
  41.9 4.9 %collective-permute-start = (f32[2,64,1,512]{3,2,1,0:T(1,128)S(1)}, f32[2,64,1,512]{3,2,1,0:T(1,128)S(1)}, u32[]{:S(2)}, u32[]{:S(2)}) collective-permute-start(f32[2,64,1,512]{3,2,1,0:T(1,128)S(1)} %get-tuple-element.33), channel_id=1, source_target_pairs={{0,1},{1,2},{2,3},{3,4},{4,5},{5,6},{6,7},{7,8},{8,9},{9,10},{10,1... | collective-permute-start | bytes 786440 | tf_op jit(solution)/shard_map/ppermute | solution.py:27
  48.8 3.2 %collective-permute-start.1 = (f32[2,1,16,512]{3,2,1,0:T(8,128)S(1)}, f32[2,1,16,512]{3,2,1,0:T(8,128)S(1)}, u32[]{:S(2)}, u32[]{:S(2)}) collective-permute-start(f32[2,1,16,512]{3,2,1,0:T(8,128)S(1)} %get-tuple-element.31), channel_id=1, source_target_pairs={{0,32},{32,64},{64,96},{1,33},{33,65},{65,97},{2,34},{34,66},{66,9... | collective-permute-start | bytes 196616 | tf_op jit(solution)/shard_map/ppermute | solution.py:27
  53.3 3.7 %collective-permute-done.2 = f32[2,1,16,512]{3,2,1,0:T(8,128)S(1)} collective-permute-done((f32[2,1,16,512]{3,2,1,0:T(8,128)S(1)}, f32[2,1,16,512]{3,2,1,0:T(8,128)S(1)}, u32[]{:S(2)}, u32[]{:S(2)}) %collective-permute-start.2) | collective-permute-done | bytes 65568 | tf_op jit(solution)/shard_map/ppermute | solution.py:28
  57.0 2.5 %select_maximum_fusion = f32[2,66,18,512]{3,2,1,0:T(8,128)S(1)} fusion(f32[2,64,1,512]{3,2,1,0:T(1,128)S(1)} %collective-permute-done.3, f32[2,64,1,512]{3,2,1,0:T(1,128)S(1)} %collective-permute-done, f32[2,1,16,512]{3,2,1,0:T(8,128)S(1)} %collective-permute-done.2, f32[1,64,16,512]{3,2,1,0:T(8,128)S(1)} %get-tuple-element.64, ...), kind=kLoop, calls=%fused_computation | loop fusion | flops 10948608 | bytes 9715712 | tf_op jit(solution)/shard_map/concatenate | solution.py:34
  60.3 5.4 %fusion.72 = (f32[64,16,511]{2,1,0:T(8,128)}, f32[64,16,511]{2,1,0:T(8,128)}, f32[64,16,511]{2,1,0:T(8,128)}, f32[64,16,511]{2,1,0:T(8,128)}) fusion(f32[66,18,512]{2,1,0:T(8,128)S(1)} %get-tuple-element.29, f32[66,18,512]{2,1,0:T(8,128)S(1)} %get-tuple-element.30), kind=kLoop, calls=%fused_computation.136 | loop fusion | bytes 16744448 | tf_op jit(solution)/shard_map/slice | solution.py:45
  65.6 8.7 %fusion.68 = (f32[64,16,512]{2,1,0:T(8,128)}, f32[64,16,512]{2,1,0:T(8,128)S(1)}, f32[64,16,512]{2,1,0:T(8,128)}) fusion(f32[64,16,511]{2,1,0:T(8,128)} %get-tuple-element.65, f32[64,16,511]{2,1,0:T(8,128)} %get-tuple-element.36, f32[64,16,511]{2,1,0:T(8,128)} %get-tuple-element.66, f32[64,16,511]{2,1,0:T(8,128)} %get-tuple-element.35, ...), kind=kLoop, calls=%fused_computation.131 | loop fusion | flops 22020096 | bytes 37732352 | tf_op jit(solution)/shard_map/mul | solution.py:104
  76.9 3.2 %collective-permute-start.5 = (f32[1,16,512]{2,1,0:T(8,128)S(1)}, f32[1,16,512]{2,1,0:T(8,128)S(1)}, u32[]{:S(2)}, u32[]{:S(2)}) collective-permute-start(f32[1,16,512]{2,1,0:T(8,128)S(1)} %get-tuple-element.61), channel_id=1, source_target_pairs={{0,32},{32,64},{64,96},{1,33},{33,65},{65,97},{2,34},{34,66},{66,9... | collective-permute-start | bytes 98312 | tf_op jit(solution)/shard_map/ppermute | solution.py:27
  83.4 5.8 %collective-permute-start.7 = (f32[64,1,512]{2,1,0:T(1,128)S(1)}, f32[64,1,512]{2,1,0:T(1,128)S(1)}, u32[]{:S(2)}, u32[]{:S(2)}) collective-permute-start(f32[64,1,512]{2,1,0:T(1,128)S(1)} %get-tuple-element.60), channel_id=1, source_target_pairs={{0,1},{1,2},{2,3},{3,4},{4,5},{5,6},{6,7},{7,8},{8,9},{9,10},{10,1... | collective-permute-start | bytes 393224 | tf_op jit(solution)/shard_map/ppermute | solution.py:27
  89.2 3.0 %fusion.83 = (f32[64,16,511]{2,1,0:T(8,128)S(1)}, f32[64,16,511]{2,1,0:T(8,128)S(1)}) fusion(f32[64,16,512]{2,1,0:T(8,128)} %get-tuple-element.26), kind=kLoop, calls=%fused_computation.147 | loop fusion | bytes 8372224 | tf_op jit(solution)/shard_map/slice | solution.py:45
  92.2 3.8 %fusion.39 = f32[64,16,512]{2,1,0:T(8,128)S(1)} fusion(f32[64,16,512]{2,1,0:T(8,128)S(1)} %copy-done.4, f32[64,16,512]{2,1,0:T(8,128)S(1)} %copy-done.7, f32[64,1,512]{2,1,0:T(1,128)S(1)} %collective-permute-done.7, f32[1,16,512]{2,1,0:T(8,128)S(1)} %collective-permute-done.4, f32[1,16,512]{2,1,0:T(8,128)S(1)} %collective-permute-done.5, ...), kind=kLoop, calls=%fused_computation.72 | loop fusion | flops 13631488 | bytes 14999552 | tf_op jit(solution)/shard_map/add | solution.py:105
  96.3 4.3 %collective-permute-start.9 = (f32[1,16,512]{2,1,0:T(8,128)S(1)}, f32[1,16,512]{2,1,0:T(8,128)S(1)}, u32[]{:S(2)}, u32[]{:S(2)}) collective-permute-start(f32[1,16,512]{2,1,0:T(8,128)S(1)} %get-tuple-element.53), channel_id=1, source_target_pairs={{0,32},{32,64},{64,96},{1,33},{33,65},{65,97},{2,34},{34,66},{66,9... | collective-permute-start | bytes 98312 | tf_op jit(solution)/shard_map/ppermute | solution.py:27
  103.8 3.6 %collective-permute-start.11 = (f32[64,1,512]{2,1,0:T(1,128)S(1)}, f32[64,1,512]{2,1,0:T(1,128)S(1)}, u32[]{:S(2)}, u32[]{:S(2)}) collective-permute-start(f32[64,1,512]{2,1,0:T(1,128)S(1)} %get-tuple-element.52), channel_id=1, source_target_pairs={{0,1},{1,2},{2,3},{3,4},{4,5},{5,6},{6,7},{7,8},{8,9},{9,10},{10,1... | collective-permute-start | bytes 393224 | tf_op jit(solution)/shard_map/ppermute | solution.py:27
  109.4 5.3 %multiply_reduce_fusion.2 = (f32[]{:T(128)}, f32[]{:T(128)}, f32[64,16,512]{2,1,0:T(8,128)}) fusion(f32[64,16,512]{2,1,0:T(8,128)S(1)} %fusion.39, f32[64,16,512]{2,1,0:T(8,128)S(1)} %copy-done.7, f32[64,16,511]{2,1,0:T(8,128)S(1)} %get-tuple-element.56, f32[64,16,511]{2,1,0:T(8,128)S(1)} %get-tuple-element.55, ...), kind=kLoop, calls=%fused_computation.122 | loop fusion | flops 13631486 | bytes 14999560 | tf_op jit(solution)/shard_map/reduce_sum | solution.py:117
  114.7 8.9 %all-reduce.27 = (f32[]{:T(128)}, f32[]{:T(128)}) all-reduce(f32[]{:T(128)} %get-tuple-element.5, f32[]{:T(128)} %get-tuple-element.4), channel_id=1, replica_groups=mesh['gx'=4,'gz_0'=4,'gz_1'=4,'gz_2'=2] {'gx'}, use_global_device_ids=true, to_apply=%region_2.3 | all-reduce | flops 2 | bytes 16 | tf_op jit(solution)/shard_map/psum | solution.py:40
  123.6 11.7 %all-reduce.25 = (f32[]{:T(128)}, f32[]{:T(128)}) all-reduce(f32[]{:T(128)} %get-tuple-element.16, f32[]{:T(128)} %get-tuple-element.17), channel_id=1, replica_groups=mesh['gx'=4,'gz_0'=4,'gz_1'=4,'gz_2'=2] {'gz_0'}, use_global_device_ids=true, to_apply=%region_3.4 | all-reduce | flops 2 | bytes 16 | tf_op jit(solution)/shard_map/psum | solution.py:40
  135.3 9.2 %all-reduce.23 = (f32[]{:T(128)}, f32[]{:T(128)}) all-reduce(f32[]{:T(128)} %get-tuple-element.12, f32[]{:T(128)} %get-tuple-element.13), channel_id=1, replica_groups=mesh['gx'=4,'gz_0'=4,'gz_1'=4,'gz_2'=2] {'gz_1'}, use_global_device_ids=true, to_apply=%region_4.5 | all-reduce | flops 2 | bytes 16 | tf_op jit(solution)/shard_map/psum | solution.py:40
  144.5 10.8 %all-reduce.29 = (f32[]{:T(128)}, f32[]{:T(128)}) all-reduce(f32[]{:T(128)} %get-tuple-element.8, f32[]{:T(128)} %get-tuple-element.9), channel_id=1, replica_groups=mesh['gx'=4,'gz_0'=4,'gz_1'=4,'gz_2'=2] {'gz_2'}, use_global_device_ids=true, to_apply=%region_5.6 | all-reduce | flops 2 | bytes 16 | tf_op jit(solution)/shard_map/psum | solution.py:40
  156.5 3.6 %fusion.67 = (f32[64,16,512]{2,1,0:T(8,128)S(1)}, f32[64,16,512]{2,1,0:T(8,128)S(1)}) fusion(f32[64,16,512]{2,1,0:T(8,128)} %copy-done, f32[64,16,512]{2,1,0:T(8,128)} %get-tuple-element.28, f32[64,16,512]{2,1,0:T(8,128)} %get-tuple-element.25, f32[]{:T(128)S(6)} %div.44), kind=kLoop, calls=%fused_computation.130 | loop fusion | flops 2097152 | bytes 10485764 | tf_op jit(solution)/shard_map/mul | solution.py:104
  163.9 2.5 %collective-permute-start.14 = (f32[64,1,512]{2,1,0:T(1,128)S(1)}, f32[64,1,512]{2,1,0:T(1,128)S(1)}, u32[]{:S(2)}, u32[]{:S(2)}) collective-permute-start(f32[64,1,512]{2,1,0:T(1,128)S(1)} %get-tuple-element.47), channel_id=1, source_target_pairs={{1,0},{2,1},{3,2},{4,3},{5,4},{6,5},{7,6},{8,7},{9,8},{10,9},{11,1... | collective-permute-start | bytes 393224 | tf_op jit(solution)/shard_map/ppermute | solution.py:28
  166.4 3.7 %collective-permute-start.15 = (f32[64,1,512]{2,1,0:T(1,128)S(1)}, f32[64,1,512]{2,1,0:T(1,128)S(1)}, u32[]{:S(2)}, u32[]{:S(2)}) collective-permute-start(f32[64,1,512]{2,1,0:T(1,128)S(1)} %get-tuple-element.48), channel_id=1, source_target_pairs={{0,1},{1,2},{2,3},{3,4},{4,5},{5,6},{6,7},{7,8},{8,9},{9,10},{10,1... | collective-permute-start | bytes 393224 | tf_op jit(solution)/shard_map/ppermute | solution.py:27
  172.0 3.8 %fusion.18 = f32[64,16,512]{2,1,0:T(8,128)S(1)} fusion(f32[64,16,512]{2,1,0:T(8,128)S(1)} %get-tuple-element.23, f32[64,16,512]{2,1,0:T(8,128)S(1)} %get-tuple-element.24, f32[64,1,512]{2,1,0:T(1,128)S(1)} %collective-permute-done.15, f32[1,16,512]{2,1,0:T(8,128)S(1)} %collective-permute-done.12, f32[1,16,512]{2,1,0:T(8,128)S(1)} %collective-permute-done.13, ...), kind=kLoop, calls=%fused_computation.35 | loop fusion | flops 13631488 | bytes 14999552 | tf_op jit(solution)/shard_map/add | solution.py:105
  176.1 4.3 %collective-permute-start.17 = (f32[1,16,512]{2,1,0:T(8,128)S(1)}, f32[1,16,512]{2,1,0:T(8,128)S(1)}, u32[]{:S(2)}, u32[]{:S(2)}) collective-permute-start(f32[1,16,512]{2,1,0:T(8,128)S(1)} %get-tuple-element.41), channel_id=1, source_target_pairs={{0,32},{32,64},{64,96},{1,33},{33,65},{65,97},{2,34},{34,66},{66,9... | collective-permute-start | bytes 98312 | tf_op jit(solution)/shard_map/ppermute | solution.py:27
  183.6 4.9 %collective-permute-start.19 = (f32[64,1,512]{2,1,0:T(1,128)S(1)}, f32[64,1,512]{2,1,0:T(1,128)S(1)}, u32[]{:S(2)}, u32[]{:S(2)}) collective-permute-start(f32[64,1,512]{2,1,0:T(1,128)S(1)} %get-tuple-element.40), channel_id=1, source_target_pairs={{0,1},{1,2},{2,3},{3,4},{4,5},{5,6},{6,7},{7,8},{8,9},{9,10},{10,1... | collective-permute-start | bytes 393224 | tf_op jit(solution)/shard_map/ppermute | solution.py:27
  190.2 5.3 %multiply_reduce_fusion = (f32[]{:T(128)}, f32[]{:T(128)}, f32[64,16,512]{2,1,0:T(8,128)}) fusion(f32[64,16,512]{2,1,0:T(8,128)S(1)} %fusion.18, f32[64,16,512]{2,1,0:T(8,128)S(1)} %get-tuple-element.24, f32[64,16,511]{2,1,0:T(8,128)S(1)} %get-tuple-element.44, f32[64,16,511]{2,1,0:T(8,128)S(1)} %get-tuple-element.43, ...), kind=kLoop, calls=%fused_computation.119 | loop fusion | flops 13631486 | bytes 14999560 | tf_op jit(solution)/shard_map/reduce_sum | solution.py:117
  195.5 9.0 %all-reduce.26 = (f32[]{:T(128)}, f32[]{:T(128)}) all-reduce(f32[]{:T(128)} %get-tuple-element.3, f32[]{:T(128)} %get-tuple-element.2), channel_id=1, replica_groups=mesh['gx'=4,'gz_0'=4,'gz_1'=4,'gz_2'=2] {'gx'}, use_global_device_ids=true, to_apply=%region_12.13 | all-reduce | flops 2 | bytes 16 | tf_op jit(solution)/shard_map/psum | solution.py:40
  204.5 9.5 %all-reduce.24 = (f32[]{:T(128)}, f32[]{:T(128)}) all-reduce(f32[]{:T(128)} %get-tuple-element.14, f32[]{:T(128)} %get-tuple-element.15), channel_id=1, replica_groups=mesh['gx'=4,'gz_0'=4,'gz_1'=4,'gz_2'=2] {'gz_0'}, use_global_device_ids=true, to_apply=%region_13.14 | all-reduce | flops 2 | bytes 16 | tf_op jit(solution)/shard_map/psum | solution.py:40
  214.1 9.1 %all-reduce.22 = (f32[]{:T(128)}, f32[]{:T(128)}) all-reduce(f32[]{:T(128)} %get-tuple-element.10, f32[]{:T(128)} %get-tuple-element.11), channel_id=1, replica_groups=mesh['gx'=4,'gz_0'=4,'gz_1'=4,'gz_2'=2] {'gz_1'}, use_global_device_ids=true, to_apply=%region_14.15 | all-reduce | flops 2 | bytes 16 | tf_op jit(solution)/shard_map/psum | solution.py:40
  223.1 10.8 %all-reduce.28 = (f32[]{:T(128)}, f32[]{:T(128)}) all-reduce(f32[]{:T(128)} %get-tuple-element.6, f32[]{:T(128)} %get-tuple-element.7), channel_id=1, replica_groups=mesh['gx'=4,'gz_0'=4,'gz_1'=4,'gz_2'=2] {'gz_2'}, use_global_device_ids=true, to_apply=%region_15.16 | all-reduce | flops 2 | bytes 16 | tf_op jit(solution)/shard_map/psum | solution.py:40
  238.4 4.4 %multiply_add_fusion = f32[64,16,512]{2,1,0:T(8,128)} fusion(f32[64,16,512]{2,1,0:T(8,128)} %copy-done.3, f32[64,16,512]{2,1,0:T(8,128)} %copy-done.2, f32[]{:T(128)S(6)} %div.45, f32[]{:T(128)S(6)} %div.47, f32[]{:T(128)S(6)} %div.44), kind=kLoop, calls=%fused_computation.118 | loop fusion | flops 2621440 | bytes 6291468 | tf_op jit(solution)/shard_map/add | solution.py:123
  (67 shorter events, 29.9 us)
Async XLA Ops:
  41.9 15.1 %collective-permute-start = (f32[2,64,1,512]{3,2,1,0:T(1,128)S(1)}, f32[2,64,1,512]{3,2,1,0:T(1,128)S(1)}, u32[]{:S(2)}, u32[]{:S(2)}) collective-permute-start(f32[2,64,1,512]{3,2,1,0:T(1,128)S(1)} %get-tuple-element.33), channel_id=1, source_target_pairs={{0,1},{1,2},{2,3},{3,4},{4,5},{5,6},{6,7},{7,8},{8,9},{9,10},{10,1... | collective-permute-start | bytes 786440 | tf_op jit(solution)/shard_map/ppermute | solution.py:27
  46.9 10.2 %collective-permute-start.3 = (f32[2,64,1,512]{3,2,1,0:T(1,128)S(1)}, f32[2,64,1,512]{3,2,1,0:T(1,128)S(1)}, u32[]{:S(2)}, u32[]{:S(2)}) collective-permute-start(f32[2,64,1,512]{3,2,1,0:T(1,128)S(1)} %get-tuple-element.34), channel_id=1, source_target_pairs={{1,0},{2,1},{3,2},{4,3},{5,4},{6,5},{7,6},{8,7},{9,8},{10,9},{11,1... | collective-permute-start | bytes 786440 | tf_op jit(solution)/shard_map/ppermute | solution.py:28
  48.8 4.5 %collective-permute-start.1 = (f32[2,1,16,512]{3,2,1,0:T(8,128)S(1)}, f32[2,1,16,512]{3,2,1,0:T(8,128)S(1)}, u32[]{:S(2)}, u32[]{:S(2)}) collective-permute-start(f32[2,1,16,512]{3,2,1,0:T(8,128)S(1)} %get-tuple-element.31), channel_id=1, source_target_pairs={{0,32},{32,64},{64,96},{1,33},{33,65},{65,97},{2,34},{34,66},{66,9... | collective-permute-start | bytes 196616 | tf_op jit(solution)/shard_map/ppermute | solution.py:27
  52.0 5.0 %collective-permute-start.2 = (f32[2,1,16,512]{3,2,1,0:T(8,128)S(1)}, f32[2,1,16,512]{3,2,1,0:T(8,128)S(1)}, u32[]{:S(2)}, u32[]{:S(2)}) collective-permute-start(f32[2,1,16,512]{3,2,1,0:T(8,128)S(1)} %get-tuple-element.32), channel_id=1, source_target_pairs={{32,0},{64,32},{96,64},{33,1},{65,33},{97,65},{34,2},{66,34},{98,6... | collective-permute-start | bytes 196616 | tf_op jit(solution)/shard_map/ppermute | solution.py:28
  74.3 35.1 %copy-start = (f32[64,16,512]{2,1,0:T(8,128)}, f32[64,16,512]{2,1,0:T(8,128)S(1)}, u32[]{:S(2)}) copy-start(f32[64,16,512]{2,1,0:T(8,128)S(1)} %get-tuple-element.27) | copy-start | bytes 6291460
  76.9 15.2 %collective-permute-start.5 = (f32[1,16,512]{2,1,0:T(8,128)S(1)}, f32[1,16,512]{2,1,0:T(8,128)S(1)}, u32[]{:S(2)}, u32[]{:S(2)}) collective-permute-start(f32[1,16,512]{2,1,0:T(8,128)S(1)} %get-tuple-element.61), channel_id=1, source_target_pairs={{0,32},{32,64},{64,96},{1,33},{33,65},{65,97},{2,34},{34,66},{66,9... | collective-permute-start | bytes 98312 | tf_op jit(solution)/shard_map/ppermute | solution.py:27
  80.2 12.0 %collective-permute-start.4 = (f32[1,16,512]{2,1,0:T(8,128)S(1)}, f32[1,16,512]{2,1,0:T(8,128)S(1)}, u32[]{:S(2)}, u32[]{:S(2)}) collective-permute-start(f32[1,16,512]{2,1,0:T(8,128)S(1)} %get-tuple-element.62), channel_id=1, source_target_pairs={{32,0},{64,32},{96,64},{33,1},{65,33},{97,65},{34,2},{66,34},{98,6... | collective-permute-start | bytes 98312 | tf_op jit(solution)/shard_map/ppermute | solution.py:28
  81.5 10.7 %collective-permute-start.6 = (f32[64,1,512]{2,1,0:T(1,128)S(1)}, f32[64,1,512]{2,1,0:T(1,128)S(1)}, u32[]{:S(2)}, u32[]{:S(2)}) collective-permute-start(f32[64,1,512]{2,1,0:T(1,128)S(1)} %get-tuple-element.59), channel_id=1, source_target_pairs={{1,0},{2,1},{3,2},{4,3},{5,4},{6,5},{7,6},{8,7},{9,8},{10,9},{11,1... | collective-permute-start | bytes 393224 | tf_op jit(solution)/shard_map/ppermute | solution.py:28
  83.4 8.8 %copy-start.4 = (f32[64,16,512]{2,1,0:T(8,128)S(1)}, f32[64,16,512]{2,1,0:T(8,128)}, u32[]{:S(2)}) copy-start(f32[64,16,512]{2,1,0:T(8,128)} %get-tuple-element.26) | copy-start | bytes 6291460
  83.4 8.8 %copy-start.7 = (f32[64,16,512]{2,1,0:T(8,128)S(1)}, f32[64,16,512]{2,1,0:T(8,128)}, u32[]{:S(2)}) copy-start(f32[64,16,512]{2,1,0:T(8,128)} %get-tuple-element.28) | copy-start | bytes 6291460
  83.4 8.8 %collective-permute-start.7 = (f32[64,1,512]{2,1,0:T(1,128)S(1)}, f32[64,1,512]{2,1,0:T(1,128)S(1)}, u32[]{:S(2)}, u32[]{:S(2)}) collective-permute-start(f32[64,1,512]{2,1,0:T(1,128)S(1)} %get-tuple-element.60), channel_id=1, source_target_pairs={{0,1},{1,2},{2,3},{3,4},{4,5},{5,6},{6,7},{7,8},{8,9},{9,10},{10,1... | collective-permute-start | bytes 393224 | tf_op jit(solution)/shard_map/ppermute | solution.py:27
  96.0 13.4 %copy-start.2 = (f32[64,16,512]{2,1,0:T(8,128)}, f32[64,16,512]{2,1,0:T(8,128)S(1)}, u32[]{:S(2)}) copy-start(f32[64,16,512]{2,1,0:T(8,128)S(1)} %fusion.39) | copy-start | bytes 6291460
  96.3 12.0 %collective-permute-start.9 = (f32[1,16,512]{2,1,0:T(8,128)S(1)}, f32[1,16,512]{2,1,0:T(8,128)S(1)}, u32[]{:S(2)}, u32[]{:S(2)}) collective-permute-start(f32[1,16,512]{2,1,0:T(8,128)S(1)} %get-tuple-element.53), channel_id=1, source_target_pairs={{0,32},{32,64},{64,96},{1,33},{33,65},{65,97},{2,34},{34,66},{66,9... | collective-permute-start | bytes 98312 | tf_op jit(solution)/shard_map/ppermute | solution.py:27
  100.6 7.7 %collective-permute-start.8 = (f32[1,16,512]{2,1,0:T(8,128)S(1)}, f32[1,16,512]{2,1,0:T(8,128)S(1)}, u32[]{:S(2)}, u32[]{:S(2)}) collective-permute-start(f32[1,16,512]{2,1,0:T(8,128)S(1)} %get-tuple-element.54), channel_id=1, source_target_pairs={{32,0},{64,32},{96,64},{33,1},{65,33},{97,65},{34,2},{66,34},{98,6... | collective-permute-start | bytes 98312 | tf_op jit(solution)/shard_map/ppermute | solution.py:28
  101.9 6.4 %collective-permute-start.10 = (f32[64,1,512]{2,1,0:T(1,128)S(1)}, f32[64,1,512]{2,1,0:T(1,128)S(1)}, u32[]{:S(2)}, u32[]{:S(2)}) collective-permute-start(f32[64,1,512]{2,1,0:T(1,128)S(1)} %get-tuple-element.51), channel_id=1, source_target_pairs={{1,0},{2,1},{3,2},{4,3},{5,4},{6,5},{7,6},{8,7},{9,8},{10,9},{11,1... | collective-permute-start | bytes 393224 | tf_op jit(solution)/shard_map/ppermute | solution.py:28
  103.8 5.6 %collective-permute-start.11 = (f32[64,1,512]{2,1,0:T(1,128)S(1)}, f32[64,1,512]{2,1,0:T(1,128)S(1)}, u32[]{:S(2)}, u32[]{:S(2)}) collective-permute-start(f32[64,1,512]{2,1,0:T(1,128)S(1)} %get-tuple-element.52), channel_id=1, source_target_pairs={{0,1},{1,2},{2,3},{3,4},{4,5},{5,6},{6,7},{7,8},{8,9},{9,10},{10,1... | collective-permute-start | bytes 393224 | tf_op jit(solution)/shard_map/ppermute | solution.py:27
  160.1 30.0 %copy-start.5 = (f32[64,16,512]{2,1,0:T(8,128)}, f32[64,16,512]{2,1,0:T(8,128)S(1)}, u32[]{:S(2)}) copy-start(f32[64,16,512]{2,1,0:T(8,128)S(1)} %get-tuple-element.24) | copy-start | bytes 6291460
  160.4 10.5 %collective-permute-start.13 = (f32[1,16,512]{2,1,0:T(8,128)S(1)}, f32[1,16,512]{2,1,0:T(8,128)S(1)}, u32[]{:S(2)}, u32[]{:S(2)}) collective-permute-start(f32[1,16,512]{2,1,0:T(8,128)S(1)} %get-tuple-element.49), channel_id=1, source_target_pairs={{0,32},{32,64},{64,96},{1,33},{33,65},{65,97},{2,34},{34,66},{66,9... | collective-permute-start | bytes 98312 | tf_op jit(solution)/shard_map/ppermute | solution.py:27
  162.6 8.4 %collective-permute-start.12 = (f32[1,16,512]{2,1,0:T(8,128)S(1)}, f32[1,16,512]{2,1,0:T(8,128)S(1)}, u32[]{:S(2)}, u32[]{:S(2)}) collective-permute-start(f32[1,16,512]{2,1,0:T(8,128)S(1)} %get-tuple-element.50), channel_id=1, source_target_pairs={{32,0},{64,32},{96,64},{33,1},{65,33},{97,65},{34,2},{66,34},{98,6... | collective-permute-start | bytes 98312 | tf_op jit(solution)/shard_map/ppermute | solution.py:28
  163.9 7.1 %collective-permute-start.14 = (f32[64,1,512]{2,1,0:T(1,128)S(1)}, f32[64,1,512]{2,1,0:T(1,128)S(1)}, u32[]{:S(2)}, u32[]{:S(2)}) collective-permute-start(f32[64,1,512]{2,1,0:T(1,128)S(1)} %get-tuple-element.47), channel_id=1, source_target_pairs={{1,0},{2,1},{3,2},{4,3},{5,4},{6,5},{7,6},{8,7},{9,8},{10,9},{11,1... | collective-permute-start | bytes 393224 | tf_op jit(solution)/shard_map/ppermute | solution.py:28
  166.4 5.6 %copy-start.1 = (f32[64,16,512]{2,1,0:T(8,128)S(1)}, f32[64,16,512]{2,1,0:T(8,128)}, u32[]{:S(2)}) copy-start(f32[64,16,512]{2,1,0:T(8,128)} %copy-done) | copy-start | bytes 6291460
  166.4 5.6 %collective-permute-start.15 = (f32[64,1,512]{2,1,0:T(1,128)S(1)}, f32[64,1,512]{2,1,0:T(1,128)S(1)}, u32[]{:S(2)}, u32[]{:S(2)}) collective-permute-start(f32[64,1,512]{2,1,0:T(1,128)S(1)} %get-tuple-element.48), channel_id=1, source_target_pairs={{0,1},{1,2},{2,3},{3,4},{4,5},{5,6},{6,7},{7,8},{8,9},{9,10},{10,1... | collective-permute-start | bytes 393224 | tf_op jit(solution)/shard_map/ppermute | solution.py:27
  175.8 14.4 %copy-start.3 = (f32[64,16,512]{2,1,0:T(8,128)}, f32[64,16,512]{2,1,0:T(8,128)S(1)}, u32[]{:S(2)}) copy-start(f32[64,16,512]{2,1,0:T(8,128)S(1)} %fusion.18) | copy-start | bytes 6291460
  176.1 13.2 %collective-permute-start.17 = (f32[1,16,512]{2,1,0:T(8,128)S(1)}, f32[1,16,512]{2,1,0:T(8,128)S(1)}, u32[]{:S(2)}, u32[]{:S(2)}) collective-permute-start(f32[1,16,512]{2,1,0:T(8,128)S(1)} %get-tuple-element.41), channel_id=1, source_target_pairs={{0,32},{32,64},{64,96},{1,33},{33,65},{65,97},{2,34},{34,66},{66,9... | collective-permute-start | bytes 98312 | tf_op jit(solution)/shard_map/ppermute | solution.py:27
  180.4 8.9 %collective-permute-start.16 = (f32[1,16,512]{2,1,0:T(8,128)S(1)}, f32[1,16,512]{2,1,0:T(8,128)S(1)}, u32[]{:S(2)}, u32[]{:S(2)}) collective-permute-start(f32[1,16,512]{2,1,0:T(8,128)S(1)} %get-tuple-element.42), channel_id=1, source_target_pairs={{32,0},{64,32},{96,64},{33,1},{65,33},{97,65},{34,2},{66,34},{98,6... | collective-permute-start | bytes 98312 | tf_op jit(solution)/shard_map/ppermute | solution.py:28
  181.7 7.6 %collective-permute-start.18 = (f32[64,1,512]{2,1,0:T(1,128)S(1)}, f32[64,1,512]{2,1,0:T(1,128)S(1)}, u32[]{:S(2)}, u32[]{:S(2)}) collective-permute-start(f32[64,1,512]{2,1,0:T(1,128)S(1)} %get-tuple-element.39), channel_id=1, source_target_pairs={{1,0},{2,1},{3,2},{4,3},{5,4},{6,5},{7,6},{8,7},{9,8},{10,9},{11,1... | collective-permute-start | bytes 393224 | tf_op jit(solution)/shard_map/ppermute | solution.py:28
  183.6 6.6 %collective-permute-start.19 = (f32[64,1,512]{2,1,0:T(1,128)S(1)}, f32[64,1,512]{2,1,0:T(1,128)S(1)}, u32[]{:S(2)}, u32[]{:S(2)}) collective-permute-start(f32[64,1,512]{2,1,0:T(1,128)S(1)} %get-tuple-element.40), channel_id=1, source_target_pairs={{0,1},{1,2},{2,3},{3,4},{4,5},{5,6},{6,7},{7,8},{8,9},{9,10},{10,1... | collective-permute-start | bytes 393224 | tf_op jit(solution)/shard_map/ppermute | solution.py:27
  238.3 4.5 %copy-start.6 = (f32[64,16,512]{2,1,0:T(8,128)S(1)}, f32[64,16,512]{2,1,0:T(8,128)}, u32[]{:S(2)}) copy-start(f32[64,16,512]{2,1,0:T(8,128)} %copy-done.5) | copy-start | bytes 6291460
  238.4 4.4 %copy-start.8 = (f32[64,16,512]{2,1,0:T(8,128)S(1)}, f32[64,16,512]{2,1,0:T(8,128)}, u32[]{:S(2)}) copy-start(f32[64,16,512]{2,1,0:T(8,128)} %get-tuple-element.25) | copy-start | bytes 6291460
  238.4 4.4 %copy-start.9 = (f32[64,16,512]{2,1,0:T(8,128)S(1)}, f32[64,16,512]{2,1,0:T(8,128)}, u32[]{:S(2)}) copy-start(f32[64,16,512]{2,1,0:T(8,128)} %get-tuple-element.22) | copy-start | bytes 6291460
where the time goes:
time: 246 us; the launch traced here: 245 us
  blocking collectives  79 us (32%)
  starting transfers between devices  56.6 us (23%)
  local copies, waits for them, and re-layouts  51.4 us (21%)
  other arithmetic  44.3 us (18%)
  between operations  6.83 us (3%)
  waiting for transfers between devices  6.71 us (3%)
    psum x8, blocking collectives, by_axis(): return functools.reduce(lax.psum, axes, array)  79 us
    ppermute x10, starting transfers between devices, with_halo(): lax.ppermute(last, axis, up)  40 us
    reshape x1, local copies, waits for them, and re-layouts, on_device(): active = jnp.broadcast_to(listed_hit[:, None, :, None, :, None], (tiles_x...  25.1 us
    ppermute x10, starting transfers between devices, with_halo(): lax.ppermute(leading, axis, [(b, a) for a, b in up])  16.7 us
    mul x2, other arithmetic, precondition(): first_pass = scale_mid * residual  12.3 us
    broadcast_in_dim x1, local copies, waits for them, and re-layouts, on_device(): jnp.broadcast_to(listed_hit[:, None, :, None, :, None], (tiles_x, TILE, t...  11.3 us
    slice x5, local copies, waits for them, and re-layouts, beside(): center[:, :, 1:]  10.8 us
    reduce_sum x2, other arithmetic, both_sums(): jnp.sum(image_of * preconditioned)  10.6 us
  transfers between devices with their start and end apart: 20, of which 4 were waited for; matrix products, arithmetic and copies ran while one was open for 2% of the time, Pallas kernels for 0%

commit v1 on v0

v1 whole, which is shorter than its diff:
```python
import functools

import jax
import jax.numpy as jnp
from jax import lax
from jax.experimental import pallas as pl
from jax.experimental.pallas import tpu as pltpu
from jax.sharding import PartitionSpec as P

MESH = pl.DeviceIdType.MESH
f32 = jnp.float32

CH, LANES = 4, 128
NX, NZ = 64, 16
X0, Z0 = 8, 5
PX, PZ = 80, 26
N_GX, N_GZ = 4, 32
SLOTS = 1024
SHIFT = 1.125
WALK = 9


def span(axis_len, origin, sign, near, far):
    if sign == 0:
        return origin, origin, axis_len
    if sign > 0:
        return origin + axis_len - far, origin - far, far - near + 1
    return origin - 1 + near, origin + axis_len - 1 + near, far - near + 1


def message_list():
    every = []
    for sx in (-1, 1):
        every.append(("ls", sx, 0, (1, 5), None, 0))
        every.append(("dv", sx, 0, (1, 4), None, 0))
    for sz in (-1, 1):
        every.append(("ls", 0, sz, None, (1, 3), 1))
        every.append(("dv", 0, sz, None, (1, 2), 1))
        every.append(("ls", 0, sz, None, (4, 5), 2))
        every.append(("dv", 0, sz, None, (3, 4), 2))
        for sx in (-1, 1):
            every.append(("ls", sx, sz, (1, 4), (1, 2), 1))
            every.append(("ls", sx, sz, (1, 2), (3, 4), 1))
            every.append(("dv", sx, sz, (1, 3), (1, 1), 1))
            every.append(("dv", sx, sz, (1, 2), (2, 3), 1))
    return every


MESSAGES = message_list()
AROUND = [(sx, sz) for sx in (-1, 0, 1) for sz in (-1, 0, 1)]


def main_kernel(
    dv_in, ls_in, ids_in,
    z0_ref, y_ref, r0_ref, w0_ref, u_ref, step_ref,
    ls, dv, air, gain, q1, q2, ids, table, sums, near_sum, far_sum,
    load_sem, send_sem, recv_sem, id_send, id_recv, ar_send, ar_recv,
):
    gx, gz = lax.axis_index("gx"), lax.axis_index("gz")
    core = lax.rem(gz, 2)
    place_z = lax.rem(gz // 2, 4)
    place_x = gz // 8

    def exists(sx, sz):
        ok = None
        for position, count, sign in ((gx, N_GX, sx), (gz, N_GZ, sz)):
            if sign:
                here = position < count - 1 if sign > 0 else position > 0
                ok = here if ok is None else jnp.logical_and(ok, here)
        return ok

    for number, (source, target) in enumerate(((ls_in, ls), (dv_in, dv))):
        for z in range(NZ):
            for c in range(CH):
                pltpu.make_async_copy(
                    source.at[:, z, pl.ds(c * LANES, LANES)],
                    target.at[c, Z0 + z, pl.ds(X0, NX)],
                    load_sem.at[number],
                ).start()
        if number == 0:
            own_ids = pltpu.make_async_copy(ids_in, ids.at[4], load_sem.at[2])
            own_ids.start()

    def own(array, number):
        region = array.at[:, pl.ds(Z0, NZ), pl.ds(X0, NX)]
        return pltpu.make_async_copy(region, region, load_sem.at[number])

    for k in range(9):
        if k != 4:
            ids[k] = jnp.full((1, SLOTS), -1, jnp.int32)

    def clear(z_first, z_count, x_first, x_count):
        def layer(z, carry):
            for array in (ls, dv):
                for c in range(CH):
                    array[c, z, pl.ds(x_first, x_count), :] = jnp.zeros((x_count, LANES), f32)
            return carry

        lax.fori_loop(z_first, z_first + z_count, layer, 0)

    pl.when(gx == 0)(lambda: clear(0, PZ, 0, X0))
    pl.when(gx == N_GX - 1)(lambda: clear(0, PZ, X0 + NX, 8))
    pl.when(gz == 0)(lambda: clear(0, Z0, 0, PX))
    pl.when(gz == N_GZ - 1)(lambda: clear(Z0 + NZ, 5, 0, PX))

    me_near = place_z * 2 + core
    me_far = gx * 4 + place_x

    def near_peer(i):
        return gx, place_x * 8 + (me_near ^ i)

    def far_peer(i):
        other = me_far ^ i
        return other // 4, lax.rem(other, 4) * 8 + me_near

    barrier = pltpu.get_barrier_semaphore()
    around = [(sx, sz) for sx, sz in AROUND if (sx, sz) != (0, 0)]
    for sx, sz in around:
        pl.when(exists(sx, sz))(
            lambda sx=sx, sz=sz: pl.semaphore_signal(
                barrier, inc=1, device_id=(gx + sx, gz + sz), device_id_type=MESH
            )
        )
    for i in range(1, 8):
        pl.semaphore_signal(barrier, inc=1, device_id=near_peer(i), device_id_type=MESH)
    for i in range(1, 16):
        pl.semaphore_signal(barrier, inc=1, device_id=far_peer(i), device_id_type=MESH)
    peers = 22
    for sx, sz in around:
        peers = peers + exists(sx, sz).astype(jnp.int32)
    pl.semaphore_wait(barrier, peers)

    def id_copy(sx, sz, peer=1):
        target = (1 - sx) * 3 + (1 - sz)
        return pltpu.make_async_remote_copy(
            ids.at[4], ids.at[target], id_send.at[target], id_recv.at[target],
            device_id=(gx + peer * sx, gz + peer * sz), device_id_type=MESH,
        )

    def layer_copy(number, peer=1):
        field, sx, sz, kx, kz, _ = MESSAGES[number]
        array = ls if field == "ls" else dv
        x_from, x_to, x_len = span(NX, X0, sx, *(kx or (0, 0)))
        z_from, z_to, z_len = span(NZ, Z0, sz, *(kz or (0, 0)))
        return pltpu.make_async_remote_copy(
            array.at[:, pl.ds(z_from, z_len), pl.ds(x_from, x_len)],
            array.at[:, pl.ds(z_to, z_len), pl.ds(x_to, x_len)],
            send_sem.at[number], recv_sem.at[number],
            device_id=(gx + peer * sx, gz + peer * sz), device_id_type=MESH,
        )

    def send(chosen):
        for number, message in enumerate(MESSAGES):
            if chosen(*message):
                _, sx, sz, _, _, _ = message
                pl.when(exists(sx, sz))(lambda number=number: layer_copy(number).start())

    def arrive(chosen):
        for number, message in enumerate(MESSAGES):
            if chosen(*message):
                _, sx, sz, _, _, _ = message
                pl.when(exists(-sx, -sz))(lambda number=number: layer_copy(number, -1).wait_recv())

    own_ids.wait()
    for sx, sz in around:
        pl.when(exists(sx, sz))(lambda sx=sx, sz=sz: id_copy(sx, sz).start())
    own(ls, 0).wait()
    send(lambda field, sx, sz, kx, kz, wave: field == "ls" and sx != 0 and sz == 0)
    send(lambda field, sx, sz, kx, kz, wave: field == "ls" and sx == 0 and wave == 1)
    send(lambda field, sx, sz, kx, kz, wave: field == "ls" and sx != 0 and sz != 0)
    own(dv, 1).wait()
    send(lambda field, sx, sz, kx, kz, wave: field == "dv" and sx == 0 and wave == 1)
    send(lambda field, sx, sz, kx, kz, wave: field == "dv" and sx != 0)
    send(lambda field, sx, sz, kx, kz, wave: wave == 2)

    row = lax.broadcasted_iota(jnp.int32, (40, 1), 0)
    row_z = (row >= 10).astype(jnp.int32) + (row >= 20).astype(jnp.int32) + (row >= 30).astype(jnp.int32)
    row_x = row - 10 * row_z
    from_device = (
        jnp.where(row_x == 0, 0, jnp.where(row_x == 9, 2, 1)) * 3
        + jnp.where(row_z == 0, 0, jnp.where(row_z == 3, 2, 1))
    )
    tile_x = jnp.where(row_x == 0, 7, jnp.where(row_x == 9, 0, row_x - 1))
    tile_z = jnp.where(row_z == 0, 1, jnp.where(row_z == 3, 0, row_z - 1))
    code = tile_x * 2 + tile_z
    for sx, sz in around:
        pl.when(exists(-sx, -sz))(lambda sx=sx, sz=sz: id_copy(sx, sz, -1).wait_recv())

    def listed(k, total):
        numbers = ids[k]
        wanted = jnp.where(from_device == k, code, -2)
        rows_hit = jnp.where((numbers >> 6) == wanted, 1.0, 0.0).astype(jnp.bfloat16)
        tile_y = lax.broadcasted_iota(jnp.int32, (64, 1), 0)
        y_hit = jnp.where((numbers & 63) == tile_y, 1.0, 0.0).astype(jnp.bfloat16)
        return total + lax.dot_general(
            rows_hit, y_hit, (((1,), (1,)), ((), ())), preferred_element_type=f32
        )

    tiles = lax.fori_loop(0, 9, listed, jnp.zeros((40, 64), f32))
    widen = lax.broadcasted_iota(jnp.int32, (64, CH * LANES), 1) >> 3
    widen = jnp.where(widen == lax.broadcasted_iota(jnp.int32, (64, CH * LANES), 0), 1.0, 0.0)
    cells = jnp.dot(tiles.astype(jnp.bfloat16), widen.astype(jnp.bfloat16), preferred_element_type=f32)
    for c in range(CH):
        table[c] = cells[:, c * LANES : (c + 1) * LANES]

    def layer_of(p):
        return jnp.where(core == 1, p, PZ - 1 - p)

    def flat(ref):
        return ref.reshape(CH, PZ * PX, LANES)

    ls_f, dv_f, air_f, gain_f, q1_f, q2_f, z0_f, y_f = map(
        flat, (ls, dv, air, gain, q1, q2, z0_ref, y_ref)
    )
    lane = lax.broadcasted_iota(jnp.int32, (8, LANES), 1)

    def rows_at(ref, r):
        return [ref[c, pl.ds(r, 8), :] for c in range(CH)]

    def beside(ref, r, middle):
        up = [pltpu.roll(v, LANES - 1, 1) for v in middle]
        down = [pltpu.roll(v, 1, 1) for v in middle]
        pieces = []
        for c in range(CH):
            after = up[c + 1] if c + 1 < CH else 0.0
            before = down[c - 1] if c > 0 else 0.0
            pieces.append(
                [
                    ref[c, pl.ds(r + 1, 8), :],
                    ref[c, pl.ds(r - 1, 8), :],
                    ref[c, pl.ds(r + PX, 8), :],
                    ref[c, pl.ds(r - PX, 8), :],
                    jnp.where(lane == LANES - 1, after, up[c]),
                    jnp.where(lane == 0, before, down[c]),
                ]
            )
        return pieces

    def added(parts):
        a, b, c, d, e, f = parts
        return ((a + b) + (c + d)) + (e + f)

    def walk(first, last, layer, carry=0):
        return lax.fori_loop(first, last + 1, lambda p, held: layer(layer_of(p), held), carry)

    def find_air(z, carry):
        base = z * PX
        row_of = 10 * (
            (z >= Z0).astype(jnp.int32) + (z >= Z0 + 8).astype(jnp.int32) + (z >= Z0 + 16).astype(jnp.int32)
        )
        for j in range(10):
            for c in range(CH):
                level = ls_f[c, pl.ds(base + 8 * j, 8), :]
                on = table[c, pl.ds(row_of + j, 1), :] > 0.5
                fluid = jnp.logical_and(level < 0, on)
                air_f[c, pl.ds(base + 8 * j, 8), :] = jnp.where(fluid, 0.0, jnp.abs(level))
        return carry

    def find_gain(z, carry):
        base = z * PX + 4
        for i in range(WALK):
            r = base + 8 * i
            middle = rows_at(air_f, r)
            level = rows_at(ls_f, r)
            value = rows_at(dv_f, r)
            for c, parts in enumerate(beside(air_f, r, middle)):
                distance = -level[c]
                most = 19.0 * distance
                extra = added([jnp.minimum(part, most) for part in parts])
                fluid = jnp.logical_and(middle[c] == 0.0, level[c] < 0)
                here = jnp.where(fluid, (2.0 / 3.0) * distance / (6.0 * distance + extra), 0.0)
                gain_f[c, pl.ds(r, 8), :] = here
                q1_f[c, pl.ds(r, 8), :] = here * value[c]
        return carry

    def stage(source, target, own_part, sign):
        def layer(z, carry):
            base = z * PX + 4
            for i in range(WALK):
                r = base + 8 * i
                middle = rows_at(source, r)
                for c, parts in enumerate(beside(source, r, middle)):
                    here = gain_f[c, pl.ds(r, 8), :] * added(parts)
                    target[c, pl.ds(r, 8), :] = own_part * middle[c] + sign * here
            return carry

        return layer

    find_z0 = stage(q1_f, z0_f, 4.0 / 3.0, 1.0)
    find_q2 = stage(z0_f, q2_f, 2.0 / 3.0, -1.0)
    find_y = stage(q2_f, y_f, 4.0 / 3.0, 1.0)

    def finish(z, held):
        base = z * PX + X0
        out = (z - Z0) * NX
        held = list(held)
        for i in range(NX // 8):
            r = base + 8 * i
            middle = rows_at(y_f, r)
            for c, parts in enumerate(beside(y_f, r, middle)):
                here = gain_f[c, pl.ds(r, 8), :]
                fluid = here > 0.0
                inverse = jnp.where(fluid, 1.0 / jnp.where(fluid, here, 1.0), 0.0)
                r0 = jnp.where(fluid, dv_f[c, pl.ds(r, 8), :], 0.0)
                w0 = inverse * q2_f[c, pl.ds(r, 8), :]
                u = inverse * ((2.0 / 3.0) * middle[c] - here * added(parts))
                z0 = z0_f[c, pl.ds(r, 8), :]
                y = middle[c]
                r0_ref[c, pl.ds(out + 8 * i, 8), :] = r0
                w0_ref[c, pl.ds(out + 8 * i, 8), :] = w0
                u_ref[c, pl.ds(out + 8 * i, 8), :] = u
                r_s, z_s, w_s = r0 - SHIFT * w0, z0 - SHIFT * y, w0 - SHIFT * u
                products = (r0 * z0, w0 * z0, r_s * z_s, w0 * z_s, w0 * y, w_s * z_s, w_s * y, u * y)
                held = [total + term for total, term in zip(held, products)]
        return tuple(held)

    from_above = lambda sz: sz == -1
    from_below = lambda sz: sz == 1
    for parity in (0, 1):
        early = from_above if parity == 0 else from_below

        @pl.when(core == parity)
        def _(early=early):
            arrive(lambda field, sx, sz, kx, kz, wave: sz != 0 and early(sz))

    arrive(lambda field, sx, sz, kx, kz, wave: sz == 0)
    walk(0, 20, find_air)
    walk(1, 19, find_gain)
    walk(2, 18, find_z0)
    walk(3, 17, find_q2)
    walk(4, 16, find_y)
    held = walk(5, 15, finish, tuple(jnp.zeros((8, LANES), f32) for _ in range(8)))

    for wave in (1, 2):
        for parity in (0, 1):
            late = from_below if parity == 0 else from_above

            @pl.when(core == parity)
            def _(late=late):
                arrive(lambda field, sx, sz, kx, kz, w: sz != 0 and w == wave and late(sz))

        if wave == 1:
            walk(21, 23, find_air)
            walk(20, 22, find_gain)
            walk(19, 21, find_z0)
            walk(18, 20, find_q2)
            walk(17, 19, find_y)
            held = walk(16, 18, finish, held)
        else:
            walk(24, 25, find_air)
            walk(23, 24, find_gain)
            walk(22, 23, find_z0)
            walk(21, 22, find_q2)
            walk(20, 21, find_y)
            held = walk(19, 20, finish, held)

    lane_row = lax.broadcasted_iota(jnp.int32, (1, LANES), 1)
    packed = jnp.zeros((1, LANES), f32)
    for k, total in enumerate(held):
        whole = jnp.sum(jnp.sum(total, axis=0, keepdims=True), axis=1, keepdims=True)
        packed = jnp.where(lane_row == k, whole, packed)

    def all_sum(value, buffer, count, peer, number):
        buffer[pl.ds(0, 1), :] = value
        for i in range(1, count):
            pltpu.make_async_remote_copy(
                buffer.at[pl.ds(0, 1)], buffer.at[pl.ds(i, 1)], ar_send.at[number], ar_recv.at[number],
                device_id=peer(i), device_id_type=MESH,
            ).start()
        every = pltpu.make_async_remote_copy(
            buffer.at[pl.ds(0, count - 1)], buffer.at[pl.ds(1, count - 1)], ar_send.at[number], ar_recv.at[number],
            device_id=peer(1), device_id_type=MESH,
        )
        every.wait_recv()
        result = jnp.sum(buffer[...], axis=0, keepdims=True)
        return result, every

    part, sent_near = all_sum(packed, near_sum, 8, near_peer, 0)
    whole, sent_far = all_sum(part, far_sum, 16, far_peer, 1)
    sums[pl.ds(0, 1), :] = whole
    gamma0, delta0, gamma_s, kappa, eta, delta_s, lam, theta = (
        sums[pl.ds(0, 1), pl.ds(k, 1)] for k in range(8)
    )
    alpha0 = gamma0 / delta0
    off = alpha0 - SHIFT
    gamma1 = gamma_s - 2.0 * off * kappa + off * off * eta
    delta1 = delta_s - 2.0 * off * lam + off * off * theta
    beta = gamma1 / gamma0
    below = delta1 - beta * gamma1 / alpha0
    alpha1 = jnp.where(below > 0, gamma1 / jnp.where(below > 0, below, 1.0), 0.0)
    for k, value in enumerate((alpha0, alpha1, beta)):
        step_ref[k] = jnp.broadcast_to(value, (8, LANES))

    for number, message in enumerate(MESSAGES):
        _, sx, sz, _, _, _ = message
        pl.when(exists(sx, sz))(lambda number=number: layer_copy(number).wait_send())
    for sx, sz in around:
        pl.when(exists(sx, sz))(lambda sx=sx, sz=sz: id_copy(sx, sz).wait_send())
    sent_near.wait_send()
    sent_far.wait_send()


def last_kernel(z0_ref, y_ref, r0_ref, w0_ref, u_ref, step_ref, p_out, r_out, p_buf, r_buf, sem):
    alpha0, alpha1, beta = step_ref[0], step_ref[1], step_ref[2]
    z0_f = z0_ref.reshape(CH, PZ * PX, LANES)
    y_f = y_ref.reshape(CH, PZ * PX, LANES)
    p_f = p_buf.reshape(CH, NZ * NX, LANES)
    r_f = r_buf.reshape(CH, NZ * NX, LANES)

    for z in range(NZ):
        def rows(i, carry, z=z):
            wide = (Z0 + z) * PX + X0 + 8 * i
            r = z * NX + 8 * i
            for c in range(CH):
                z0 = z0_f[c, pl.ds(wide, 8), :]
                z1 = z0 - alpha0 * y_f[c, pl.ds(wide, 8), :]
                p_f[c, pl.ds(r, 8), :] = alpha0 * z0 + alpha1 * (z1 + beta * z0)
                w0 = w0_ref[c, pl.ds(r, 8), :]
                w1 = w0 - alpha0 * u_ref[c, pl.ds(r, 8), :]
                r1 = r0_ref[c, pl.ds(r, 8), :] - alpha0 * w0
                r_f[c, pl.ds(r, 8), :] = r1 - alpha1 * (w1 + beta * w0)
            return carry

        lax.fori_loop(0, NX // 8, rows, 0, unroll=True)
        for number, (buffer, target) in enumerate(((p_buf, p_out), (r_buf, r_out))):
            for c in range(CH):
                pltpu.make_async_copy(
                    buffer.at[c, z], target.at[:, z, pl.ds(c * LANES, LANES)], sem.at[number]
                ).start()
    for number, buffer in enumerate((p_buf, r_buf)):
        pltpu.make_async_copy(buffer, buffer, sem.at[number]).wait()


def on_device(divergence, level_set, tile_ids):
    extended = (CH, PZ, PX, LANES)
    block = (CH, NZ * NX, LANES)
    held = pl.pallas_call(
        main_kernel,
        out_shape=[pltpu.VMEM(extended, f32)] * 2 + [pltpu.VMEM(block, f32)] * 3 + [pltpu.VMEM((3, 8, LANES), f32)],
        in_specs=[pl.BlockSpec(memory_space=pltpu.HBM)] * 3,
        out_specs=[pl.BlockSpec(memory_space=pltpu.VMEM)] * 6,
        scratch_shapes=[
            pltpu.VMEM(extended, f32), pltpu.VMEM(extended, f32), pltpu.VMEM(extended, f32),
            pltpu.VMEM(extended, f32), pltpu.VMEM(extended, f32), pltpu.VMEM(extended, f32),
            pltpu.VMEM((9, 1, SLOTS), jnp.int32),
            pltpu.VMEM((CH, 40, LANES), f32),
            pltpu.VMEM((8, LANES), f32),
            pltpu.VMEM((8, LANES), f32),
            pltpu.VMEM((16, LANES), f32),
            pltpu.SemaphoreType.DMA((3,)),
            pltpu.SemaphoreType.DMA((len(MESSAGES),)),
            pltpu.SemaphoreType.DMA((len(MESSAGES),)),
            pltpu.SemaphoreType.DMA((9,)),
            pltpu.SemaphoreType.DMA((9,)),
            pltpu.SemaphoreType.DMA((2,)),
            pltpu.SemaphoreType.DMA((2,)),
        ],
        compiler_params=pltpu.CompilerParams(
            collective_id=0, has_side_effects=True, vmem_limit_bytes=36 * 2**20
        ),
        name="solve",
    )(*(pltpu.with_memory_space_constraint(array, pltpu.HBM) for array in (divergence, level_set, tile_ids)))
    return pl.pallas_call(
        last_kernel,
        out_shape=[jax.ShapeDtypeStruct(divergence.shape, f32)] * 2,
        in_specs=[pl.BlockSpec(memory_space=pltpu.VMEM)] * 6,
        out_specs=[pl.BlockSpec(memory_space=pl.ANY)] * 2,
        scratch_shapes=[
            pltpu.VMEM((CH, NZ, NX, LANES), f32),
            pltpu.VMEM((CH, NZ, NX, LANES), f32),
            pltpu.SemaphoreType.DMA((2,)),
        ],
        compiler_params=pltpu.CompilerParams(vmem_limit_bytes=12 * 2**20),
        name="update",
    )(*held)


def solution(mesh):
    return jax.shard_map(
        on_device,
        mesh=mesh,
        in_specs=(P("gx", "gz", None), P("gx", "gz", None), P("gx", "gz")),
        out_specs=(P("gx", "gz", None), P("gx", "gz", None)),
        check_vma=False,
    )
```

time: 246 us -> 47.1 us (0.19)
  blocking collectives: 79 us -> 0 us
  starting transfers between devices: 56.6 us -> 0 us
  local copies, waits for them, and re-layouts: 51.4 us -> 0 us
  Pallas kernels: 0 us -> 46.1 us
  other arithmetic: 44.3 us -> 0 us
  waiting for transfers between devices: 6.71 us -> 0 us
  between operations: 6.83 us -> 0.64 us
    psum x8 -> x0, blocking collectives: 79 us -> none  [by_axis(): return functools.reduce(lax.psum, axes, array)]
    ppermute x20 -> x0, starting transfers between devices: 56.6 us -> none  [the longest x10 40 us: with_halo(): lax.ppermute(last, axis, up)]
    pallas_call x0 -> x2, Pallas kernels: none -> 46.1 us  [the longest x1 44.1 us: on_device(): pl.pallas_call(main_kernel, out_shape=[pltpu.VMEM(extended, f32)] * 2 + [...]
    reshape x1 -> x0, local copies, waits for them, and re-layouts: 25.1 us -> none  [on_device(): active = jnp.broadcast_to(listed_hit[:, None, :, None, :, None], (tiles_x...]
    slice x13 -> x0, local copies, waits for them, and re-layouts: 14.2 us -> none  [the longest x5 10.8 us: beside(): center[:, :, 1:]]
    mul x2 -> x0, other arithmetic: 12.3 us -> none  [precondition(): first_pass = scale_mid * residual]
    add x3 -> x0, other arithmetic: 12 us -> none  [the longest x2 7.55 us: precondition(): second_pass = first_pass + scale_mid * (residual - operate(first_pass))]
    broadcast_in_dim x1 -> x0, local copies, waits for them, and re-layouts: 11.3 us -> none  [on_device(): jnp.broadcast_to(listed_hit[:, None, :, None, :, None], (tiles_x, TILE, t...]
  transfers between devices with their start and end apart: 20 -> 0, of which waited for: 4 -> 0; matrix products, arithmetic and copies ran while one was open for 2% -> 0% of each run, Pallas kernels for 0% -> 0%
where the time goes in v1:
time: 47.1 us; the launch traced here: 46.7 us
  Pallas kernels  46.1 us (98%)
  between operations  0.64 us (1%)
    pallas_call x1, Pallas kernels, on_device(): pl.pallas_call(main_kernel, out_shape=[pltpu.VMEM(extended, f32)] * 2 + [...  44.1 us
    pallas_call x1, Pallas kernels, on_device(): pl.pallas_call(last_kernel, out_shape=[jax.ShapeDtypeStruct(divergence.sh...  2.01 us

profile of v1, /device:TPU:1, one launch (start us, length us, event | category | flops | bytes accessed | tf_op | source)
XLA Modules:
  0.0 46.7 jit_solution(8790346753087071975)
XLA Ops:
  0.6 44.1 %solve.1 = (f32[4,26,80,128]{3,2,1,0:T(8,128)S(1)}, f32[4,26,80,128]{3,2,1,0:T(8,128)S(1)}, f32[4,1024,128]{2,1,0:T(8,128)S(1)}, f32[4,1024,128]{2,1,0:T(8,128)S...) custom-call(f32[64,16,512]{2,1,0:T(8,128)} %dv_in.1, f32[64,16,512]{2,1,0:T(8,128)} %ls_in.1, s32[1,1024]{1,0:T(1,128)} %ids_in.1), custom_call_target="tpu_custom_call" | custom-call | tf_op jit(solution)/shard_map/solve/pallas_call | solution.py:437
  44.7 2.0 %update.1 = (f32[64,16,512]{2,1,0:T(8,128)}, f32[64,16,512]{2,1,0:T(8,128)}) custom-call(f32[4,26,80,128]{3,2,1,0:T(8,128)S(1)} %get-tuple-element.8.z0_ref, f32[4,26,80,128]{3,2,1,0:T(8,128)S(1)} %get-tuple-element.9.y_ref, f32[4,1024,128]{2,1,0:T(8,128)S(1)} %get-tuple-element.10.r0_ref, f32[4,1024,128]{2,1,0:T(8,128)S(1)} %get-tuple-element.11.w0_ref, ...), custom_call_target="tpu_custom_call" | custom-call | tf_op jit(solution)/shard_map/update/pallas_call | solution.py:463

commit v2 on v1

--- a/solution.py
+++ b/solution.py
@@ -69,21 +69,24 @@
                 ok = here if ok is None else jnp.logical_and(ok, here)
         return ok
 
-    for number, (source, target) in enumerate(((ls_in, ls), (dv_in, dv))):
-        for z in range(NZ):
-            for c in range(CH):
-                pltpu.make_async_copy(
-                    source.at[:, z, pl.ds(c * LANES, LANES)],
-                    target.at[c, Z0 + z, pl.ds(X0, NX)],
-                    load_sem.at[number],
-                ).start()
-        if number == 0:
-            own_ids = pltpu.make_async_copy(ids_in, ids.at[4], load_sem.at[2])
-            own_ids.start()
-
-    def own(array, number):
-        region = array.at[:, pl.ds(Z0, NZ), pl.ds(X0, NX)]
-        return pltpu.make_async_copy(region, region, load_sem.at[number])
+    own_ids = pltpu.make_async_copy(ids_in, ids.at[4], load_sem.at[6])
+    own_ids.start()
+    parts = ((0, 5), (11, 5), (5, 6))
+    for field, (source, target) in enumerate(((ls_in, ls), (dv_in, dv))):
+        for part, (first, count) in enumerate(parts):
+            for z in range(first, first + count):
+                for c in range(CH):
+                    pltpu.make_async_copy(
+                        source.at[:, z, pl.ds(c * LANES, LANES)],
+                        target.at[c, Z0 + z, pl.ds(X0, NX)],
+                        load_sem.at[field * 3 + part],
+                    ).start()
+
+    def loaded(array, field, chosen):
+        for part in chosen:
+            first, count = parts[part]
+            region = array.at[:, pl.ds(Z0 + first, count), pl.ds(X0, NX)]
+            pltpu.make_async_copy(region, region, load_sem.at[field * 3 + part]).wait()
 
     for k in range(9):
         if k != 4:
@@ -164,13 +167,16 @@
     own_ids.wait()
     for sx, sz in around:
         pl.when(exists(sx, sz))(lambda sx=sx, sz=sz: id_copy(sx, sz).start())
-    own(ls, 0).wait()
+    loaded(ls, 0, (0, 1))
+    send(lambda field, sx, sz, kx, kz, wave: field == "ls" and sx == 0 and wave == 1)
+    loaded(ls, 0, (2,))
     send(lambda field, sx, sz, kx, kz, wave: field == "ls" and sx != 0 and sz == 0)
-    send(lambda field, sx, sz, kx, kz, wave: field == "ls" and sx == 0 and wave == 1)
     send(lambda field, sx, sz, kx, kz, wave: field == "ls" and sx != 0 and sz != 0)
-    own(dv, 1).wait()
+    loaded(dv, 1, (0, 1))
     send(lambda field, sx, sz, kx, kz, wave: field == "dv" and sx == 0 and wave == 1)
-    send(lambda field, sx, sz, kx, kz, wave: field == "dv" and sx != 0)
+    loaded(dv, 1, (2,))
+    send(lambda field, sx, sz, kx, kz, wave: field == "dv" and sx != 0 and sz == 0)
+    send(lambda field, sx, sz, kx, kz, wave: field == "dv" and sx != 0 and sz != 0)
     send(lambda field, sx, sz, kx, kz, wave: wave == 2)
 
     row = lax.broadcasted_iota(jnp.int32, (40, 1), 0)
@@ -183,8 +189,6 @@
     tile_x = jnp.where(row_x == 0, 7, jnp.where(row_x == 9, 0, row_x - 1))
     tile_z = jnp.where(row_z == 0, 1, jnp.where(row_z == 3, 0, row_z - 1))
     code = tile_x * 2 + tile_z
-    for sx, sz in around:
-        pl.when(exists(-sx, -sz))(lambda sx=sx, sz=sz: id_copy(sx, sz, -1).wait_recv())
 
     def listed(k, total):
         numbers = ids[k]
@@ -196,12 +200,15 @@
             rows_hit, y_hit, (((1,), (1,)), ((), ())), preferred_element_type=f32
         )
 
-    tiles = lax.fori_loop(0, 9, listed, jnp.zeros((40, 64), f32))
     widen = lax.broadcasted_iota(jnp.int32, (64, CH * LANES), 1) >> 3
     widen = jnp.where(widen == lax.broadcasted_iota(jnp.int32, (64, CH * LANES), 0), 1.0, 0.0)
-    cells = jnp.dot(tiles.astype(jnp.bfloat16), widen.astype(jnp.bfloat16), preferred_element_type=f32)
-    for c in range(CH):
-        table[c] = cells[:, c * LANES : (c + 1) * LANES]
+    widen = widen.astype(jnp.bfloat16)
+
+    def fill_table(first, last):
+        tiles = lax.fori_loop(first, last, listed, jnp.zeros((40, 64), f32))
+        cells = jnp.dot(tiles.astype(jnp.bfloat16), widen, preferred_element_type=f32)
+        for c in range(CH):
+            table[c] = cells[:, c * LANES : (c + 1) * LANES]
 
     def layer_of(p):
         return jnp.where(core == 1, p, PZ - 1 - p)
@@ -240,37 +247,64 @@
         a, b, c, d, e, f = parts
         return ((a + b) + (c + d)) + (e + f)
 
-    def walk(first, last, layer, carry=0):
-        return lax.fori_loop(first, last + 1, lambda p, held: layer(layer_of(p), held), carry)
-
-    def find_air(z, carry):
-        base = z * PX
-        row_of = 10 * (
-            (z >= Z0).astype(jnp.int32) + (z >= Z0 + 8).astype(jnp.int32) + (z >= Z0 + 16).astype(jnp.int32)
-        )
-        for j in range(10):
+    def walk(first, last, layer, held=0, group=3):
+        rounds = (last - first + 1) // group
+
+        def some(q, held):
+            for step in range(group):
+                held = layer(layer_of(first + q * group + step), held)
+            return held
+
+        if rounds > 1:
+            held = lax.fori_loop(0, rounds, some, held)
+            first = first + rounds * group
+        for p in range(first, last + 1):
+            held = layer(layer_of(p), held)
+        return held
+
+    def find_air(columns):
+        def layer(z, carry):
+            base = z * PX
+            row_of = 10 * (
+                (z >= Z0).astype(jnp.int32)
+                + (z >= Z0 + 8).astype(jnp.int32)
+                + (z >= Z0 + 16).astype(jnp.int32)
+            )
+            for j in columns:
+                for c in range(CH):
+                    level = ls_f[c, pl.ds(base + 8 * j, 8), :]
+                    on = table[c, pl.ds(row_of + j, 1), :] > 0.5
+                    fluid = jnp.logical_and(level < 0, on)
+                    air_f[c, pl.ds(base + 8 * j, 8), :] = jnp.where(fluid, 0.0, jnp.abs(level))
+            return carry
+
+        return layer
+
+    def find_gain(columns, with_q1=True):
+        def layer(z, carry):
+            base = z * PX + 4
+            for i in columns:
+                r = base + 8 * i
+                middle = rows_at(air_f, r)
+                for c, parts in enumerate(beside(air_f, r, middle)):
+                    level = ls_f[c, pl.ds(r, 8), :]
+                    distance = -level
+                    most = 19.0 * distance
+                    extra = added([jnp.minimum(part, most) for part in parts])
+                    fluid = jnp.logical_and(middle[c] == 0.0, level < 0)
+                    here = jnp.where(fluid, (2.0 / 3.0) * distance / (6.0 * distance + extra), 0.0)
+                    gain_f[c, pl.ds(r, 8), :] = here
+                    if with_q1:
+                        q1_f[c, pl.ds(r, 8), :] = here * dv_f[c, pl.ds(r, 8), :]
+            return carry
+
+        return layer
+
+    def find_q1(z, carry):
+        for i in (0, WALK - 1):
+            r = z * PX + 4 + 8 * i
             for c in range(CH):
-                level = ls_f[c, pl.ds(base + 8 * j, 8), :]
-                on = table[c, pl.ds(row_of + j, 1), :] > 0.5
-                fluid = jnp.logical_and(level < 0, on)
-                air_f[c, pl.ds(base + 8 * j, 8), :] = jnp.where(fluid, 0.0, jnp.abs(level))
-        return carry
-
-    def find_gain(z, carry):
-        base = z * PX + 4
-        for i in range(WALK):
-            r = base + 8 * i
-            middle = rows_at(air_f, r)
-            level = rows_at(ls_f, r)
-            value = rows_at(dv_f, r)
-            for c, parts in enumerate(beside(air_f, r, middle)):
-                distance = -level[c]
-                most = 19.0 * distance
-                extra = added([jnp.minimum(part, most) for part in parts])
-                fluid = jnp.logical_and(middle[c] == 0.0, level[c] < 0)
-                here = jnp.where(fluid, (2.0 / 3.0) * distance / (6.0 * distance + extra), 0.0)
-                gain_f[c, pl.ds(r, 8), :] = here
-                q1_f[c, pl.ds(r, 8), :] = here * value[c]
+                q1_f[c, pl.ds(r, 8), :] = gain_f[c, pl.ds(r, 8), :] * dv_f[c, pl.ds(r, 8), :]
         return carry
 
     def stage(source, target, own_part, sign):
@@ -310,49 +344,63 @@
                 w0_ref[c, pl.ds(out + 8 * i, 8), :] = w0
                 u_ref[c, pl.ds(out + 8 * i, 8), :] = u
                 r_s, z_s, w_s = r0 - SHIFT * w0, z0 - SHIFT * y, w0 - SHIFT * u
-                products = (r0 * z0, w0 * z0, r_s * z_s, w0 * z_s, w0 * y, w_s * z_s, w_s * y, u * y)
+                products = (r0 * z0, w0 * z0, w0 * y, u * y, r_s * z_s, w_s * z_s)
                 held = [total + term for total, term in zip(held, products)]
         return tuple(held)
 
     from_above = lambda sz: sz == -1
     from_below = lambda sz: sz == 1
-    for parity in (0, 1):
-        early = from_above if parity == 0 else from_below
-
-        @pl.when(core == parity)
-        def _(early=early):
-            arrive(lambda field, sx, sz, kx, kz, wave: sz != 0 and early(sz))
-
-    arrive(lambda field, sx, sz, kx, kz, wave: sz == 0)
-    walk(0, 20, find_air)
-    walk(1, 19, find_gain)
+
+    def arrive_at(side_of_even, side_of_odd, chosen):
+        for parity, side in ((0, side_of_even), (1, side_of_odd)):
+
+            @pl.when(core == parity)
+            def _(side=side):
+                arrive(lambda field, sx, sz, kx, kz, wave: side(sz) and chosen(field, sx, wave))
+
+    def arrive_early(chosen):
+        arrive_at(from_above, from_below, chosen)
+
+    def arrive_late(chosen):
+        arrive_at(from_below, from_above, chosen)
+
+    every_column, inner = range(10), range(1, 9)
+    edges, between = (0, WALK - 1), range(1, WALK - 1)
+    fill_table(4, 5)
+    walk(5, 20, find_air(inner))
+    for sx, sz in around:
+        pl.when(exists(-sx, -sz))(lambda sx=sx, sz=sz: id_copy(sx, sz, -1).wait_recv())
+    fill_table(0, 9)
+    arrive_early(lambda field, sx, wave: sx == 0)
+    walk(0, 4, find_air(inner))
+    walk(1, 19, find_gain(between))
+    arrive(lambda field, sx, sz, kx, kz, wave: sz == 0 and field == "ls")
+    arrive_early(lambda field, sx, wave: sx != 0 and field == "ls")
+    walk(0, 20, find_air((0, 9)))
+    walk(1, 19, find_gain(edges, False))
+    arrive(lambda field, sx, sz, kx, kz, wave: sz == 0 and field == "dv")
+    arrive_early(lambda field, sx, wave: sx != 0 and field == "dv")
+    walk(1, 19, find_q1)
     walk(2, 18, find_z0)
     walk(3, 17, find_q2)
     walk(4, 16, find_y)
-    held = walk(5, 15, finish, tuple(jnp.zeros((8, LANES), f32) for _ in range(8)))
-
-    for wave in (1, 2):
-        for parity in (0, 1):
-            late = from_below if parity == 0 else from_above
-
-            @pl.when(core == parity)
-            def _(late=late):
-                arrive(lambda field, sx, sz, kx, kz, w: sz != 0 and w == wave and late(sz))
-
-        if wave == 1:
-            walk(21, 23, find_air)
-            walk(20, 22, find_gain)
-            walk(19, 21, find_z0)
-            walk(18, 20, find_q2)
-            walk(17, 19, find_y)
-            held = walk(16, 18, finish, held)
-        else:
-            walk(24, 25, find_air)
-            walk(23, 24, find_gain)
-            walk(22, 23, find_z0)
-            walk(21, 22, find_q2)
-            walk(20, 21, find_y)
-            held = walk(19, 20, finish, held)
+    held = walk(5, 15, finish, tuple(jnp.zeros((8, LANES), f32) for _ in range(6)))
+
+    arrive_late(lambda field, sx, wave: wave == 1)
+    walk(21, 23, find_air(every_column))
+    walk(20, 22, find_gain(range(WALK)))
+    walk(19, 21, find_z0)
+    walk(18, 20, find_q2)
+    walk(17, 19, find_y)
+    held = walk(16, 18, finish, held)
+
+    arrive_late(lambda field, sx, wave: wave == 2)
+    walk(24, 25, find_air(every_column))
+    walk(23, 24, find_gain(range(WALK)))
+    walk(22, 23, find_z0)
+    walk(21, 22, find_q2)
+    walk(20, 21, find_y)
+    held = walk(19, 20, finish, held)
 
     lane_row = lax.broadcasted_iota(jnp.int32, (1, LANES), 1)
     packed = jnp.zeros((1, LANES), f32)
@@ -378,11 +426,10 @@
     part, sent_near = all_sum(packed, near_sum, 8, near_peer, 0)
     whole, sent_far = all_sum(part, far_sum, 16, far_peer, 1)
     sums[pl.ds(0, 1), :] = whole
-    gamma0, delta0, gamma_s, kappa, eta, delta_s, lam, theta = (
-        sums[pl.ds(0, 1), pl.ds(k, 1)] for k in range(8)
-    )
+    gamma0, delta0, eta, theta, gamma_s, delta_s = (sums[pl.ds(0, 1), pl.ds(k, 1)] for k in range(6))
     alpha0 = gamma0 / delta0
     off = alpha0 - SHIFT
+    kappa, lam = delta0 - SHIFT * eta, eta - SHIFT * theta
     gamma1 = gamma_s - 2.0 * off * kappa + off * off * eta
     delta1 = delta_s - 2.0 * off * lam + off * off * theta
     beta = gamma1 / gamma0
@@ -447,7 +494,7 @@
             pltpu.VMEM((8, LANES), f32),
             pltpu.VMEM((8, LANES), f32),
             pltpu.VMEM((16, LANES), f32),
-            pltpu.SemaphoreType.DMA((3,)),
+            pltpu.SemaphoreType.DMA((7,)),
             pltpu.SemaphoreType.DMA((len(MESSAGES),)),
             pltpu.SemaphoreType.DMA((len(MESSAGES),)),
             pltpu.SemaphoreType.DMA((9,)),

time: 47.1 us -> 39.9 us (0.85)
  Pallas kernels: 46.1 us -> 39 us
    pallas_call x1, Pallas kernels: 44.1 us -> 37 us  [on_device(): pl.pallas_call(main_kernel, out_shape=[pltpu.VMEM(extended, f32)] * 2 + [...]
where the time goes in v2:
time: 39.9 us; the launch traced here: 39.6 us
  Pallas kernels  39 us (98%)
  between operations  0.64 us (2%)
    pallas_call x1, Pallas kernels, on_device(): pl.pallas_call(main_kernel, out_shape=[pltpu.VMEM(extended, f32)] * 2 + [...  37 us
    pallas_call x1, Pallas kernels, on_device(): pl.pallas_call(last_kernel, out_shape=[jax.ShapeDtypeStruct(divergence.sh...  2.01 us

profile of v2, /device:TPU:1, one launch (start us, length us, event | category | flops | bytes accessed | tf_op | source)
XLA Modules:
  0.0 39.6 jit_solution(14290229878294411905)
XLA Ops:
  0.6 37.0 %solve.1 = (f32[4,26,80,128]{3,2,1,0:T(8,128)S(1)}, f32[4,26,80,128]{3,2,1,0:T(8,128)S(1)}, f32[4,1024,128]{2,1,0:T(8,128)S(1)}, f32[4,1024,128]{2,1,0:T(8,128)S...) custom-call(f32[64,16,512]{2,1,0:T(8,128)} %dv_in.1, f32[64,16,512]{2,1,0:T(8,128)} %ls_in.1, s32[1,1024]{1,0:T(1,128)} %ids_in.1), custom_call_target="tpu_custom_call" | custom-call | tf_op jit(solution)/shard_map/solve/pallas_call | solution.py:484
  37.6 2.0 %update.1 = (f32[64,16,512]{2,1,0:T(8,128)}, f32[64,16,512]{2,1,0:T(8,128)}) custom-call(f32[4,26,80,128]{3,2,1,0:T(8,128)S(1)} %get-tuple-element.8.z0_ref, f32[4,26,80,128]{3,2,1,0:T(8,128)S(1)} %get-tuple-element.9.y_ref, f32[4,1024,128]{2,1,0:T(8,128)S(1)} %get-tuple-element.10.r0_ref, f32[4,1024,128]{2,1,0:T(8,128)S(1)} %get-tuple-element.11.w0_ref, ...), custom_call_target="tpu_custom_call" | custom-call | tf_op jit(solution)/shard_map/update/pallas_call | solution.py:510

commit v3 on v2

--- a/solution.py
+++ b/solution.py
@@ -34,10 +34,10 @@
         every.append(("ls", sx, 0, (1, 5), None, 0))
         every.append(("dv", sx, 0, (1, 4), None, 0))
     for sz in (-1, 1):
-        every.append(("ls", 0, sz, None, (1, 3), 1))
-        every.append(("dv", 0, sz, None, (1, 2), 1))
-        every.append(("ls", 0, sz, None, (4, 5), 2))
-        every.append(("dv", 0, sz, None, (3, 4), 2))
+        every.append(("ls", 0, sz, None, (1, 4), 1))
+        every.append(("dv", 0, sz, None, (1, 3), 1))
+        every.append(("ls", 0, sz, None, (5, 5), 2))
+        every.append(("dv", 0, sz, None, (4, 4), 2))
         for sx in (-1, 1):
             every.append(("ls", sx, sz, (1, 4), (1, 2), 1))
             every.append(("ls", sx, sz, (1, 2), (3, 4), 1))
@@ -53,7 +53,7 @@
 def main_kernel(
     dv_in, ls_in, ids_in,
     z0_ref, y_ref, r0_ref, w0_ref, u_ref, step_ref,
-    ls, dv, air, gain, q1, q2, ids, table, sums, near_sum, far_sum,
+    ls, dv, air, dist, gain, q1, q2, ids, table, sums, near_sum, far_sum,
     load_sem, send_sem, recv_sem, id_send, id_recv, ar_send, ar_recv,
 ):
     gx, gz = lax.axis_index("gx"), lax.axis_index("gz")
@@ -69,6 +69,46 @@
                 ok = here if ok is None else jnp.logical_and(ok, here)
         return ok
 
+    for k in range(9):
+        if k != 4:
+            ids[k] = jnp.full((1, SLOTS), -1, jnp.int32)
+
+    def clear(z_first, z_count, x_first, x_count):
+        def layer(z, carry):
+            for array in (ls, dv):
+                for c in range(CH):
+                    array[c, z, pl.ds(x_first, x_count), :] = jnp.zeros((x_count, LANES), f32)
+            return carry
+
+        lax.fori_loop(z_first, z_first + z_count, layer, 0)
+
+    pl.when(gx == 0)(lambda: clear(0, PZ, 0, X0))
+    pl.when(gx == N_GX - 1)(lambda: clear(0, PZ, X0 + NX, 8))
+    pl.when(gz == 0)(lambda: clear(0, Z0, 0, PX))
+    pl.when(gz == N_GZ - 1)(lambda: clear(Z0 + NZ, 5, 0, PX))
+
+    me_near = place_z * 2 + core
+    me_far = gx * 4 + place_x
+
+    def near_peer(i):
+        return gx, place_x * 8 + (me_near ^ i)
+
+    def far_peer(i):
+        other = me_far ^ i
+        return other // 4, lax.rem(other, 4) * 8 + me_near
+
+    barrier = pltpu.get_barrier_semaphore()
+    around = [(sx, sz) for sx, sz in AROUND if (sx, sz) != (0, 0)]
+    for sx, sz in around:
+        pl.when(exists(sx, sz))(
+            lambda sx=sx, sz=sz: pl.semaphore_signal(
+                barrier, inc=1, device_id=(gx + sx, gz + sz), device_id_type=MESH
+            )
+        )
+    for i in range(1, 8):
+        pl.semaphore_signal(barrier, inc=1, device_id=near_peer(i), device_id_type=MESH)
+    for i in range(1, 16):
+        pl.semaphore_signal(barrier, inc=1, device_id=far_peer(i), device_id_type=MESH)
     own_ids = pltpu.make_async_copy(ids_in, ids.at[4], load_sem.at[6])
     own_ids.start()
     parts = ((0, 5), (11, 5), (5, 6))
@@ -88,46 +128,6 @@
             region = array.at[:, pl.ds(Z0 + first, count), pl.ds(X0, NX)]
             pltpu.make_async_copy(region, region, load_sem.at[field * 3 + part]).wait()
 
-    for k in range(9):
-        if k != 4:
-            ids[k] = jnp.full((1, SLOTS), -1, jnp.int32)
-
-    def clear(z_first, z_count, x_first, x_count):
-        def layer(z, carry):
-            for array in (ls, dv):
-                for c in range(CH):
-                    array[c, z, pl.ds(x_first, x_count), :] = jnp.zeros((x_count, LANES), f32)
-            return carry
-
-        lax.fori_loop(z_first, z_first + z_count, layer, 0)
-
-    pl.when(gx == 0)(lambda: clear(0, PZ, 0, X0))
-    pl.when(gx == N_GX - 1)(lambda: clear(0, PZ, X0 + NX, 8))
-    pl.when(gz == 0)(lambda: clear(0, Z0, 0, PX))
-    pl.when(gz == N_GZ - 1)(lambda: clear(Z0 + NZ, 5, 0, PX))
-
-    me_near = place_z * 2 + core
-    me_far = gx * 4 + place_x
-
-    def near_peer(i):
-        return gx, place_x * 8 + (me_near ^ i)
-
-    def far_peer(i):
-        other = me_far ^ i
-        return other // 4, lax.rem(other, 4) * 8 + me_near
-
-    barrier = pltpu.get_barrier_semaphore()
-    around = [(sx, sz) for sx, sz in AROUND if (sx, sz) != (0, 0)]
-    for sx, sz in around:
-        pl.when(exists(sx, sz))(
-            lambda sx=sx, sz=sz: pl.semaphore_signal(
-                barrier, inc=1, device_id=(gx + sx, gz + sz), device_id_type=MESH
-            )
-        )
-    for i in range(1, 8):
-        pl.semaphore_signal(barrier, inc=1, device_id=near_peer(i), device_id_type=MESH)
-    for i in range(1, 16):
-        pl.semaphore_signal(barrier, inc=1, device_id=far_peer(i), device_id_type=MESH)
     peers = 22
     for sx, sz in around:
         peers = peers + exists(sx, sz).astype(jnp.int32)
@@ -172,12 +172,6 @@
     loaded(ls, 0, (2,))
     send(lambda field, sx, sz, kx, kz, wave: field == "ls" and sx != 0 and sz == 0)
     send(lambda field, sx, sz, kx, kz, wave: field == "ls" and sx != 0 and sz != 0)
-    loaded(dv, 1, (0, 1))
-    send(lambda field, sx, sz, kx, kz, wave: field == "dv" and sx == 0 and wave == 1)
-    loaded(dv, 1, (2,))
-    send(lambda field, sx, sz, kx, kz, wave: field == "dv" and sx != 0 and sz == 0)
-    send(lambda field, sx, sz, kx, kz, wave: field == "dv" and sx != 0 and sz != 0)
-    send(lambda field, sx, sz, kx, kz, wave: wave == 2)
 
     row = lax.broadcasted_iota(jnp.int32, (40, 1), 0)
     row_z = (row >= 10).astype(jnp.int32) + (row >= 20).astype(jnp.int32) + (row >= 30).astype(jnp.int32)
@@ -216,8 +210,8 @@
     def flat(ref):
         return ref.reshape(CH, PZ * PX, LANES)
 
-    ls_f, dv_f, air_f, gain_f, q1_f, q2_f, z0_f, y_f = map(
-        flat, (ls, dv, air, gain, q1, q2, z0_ref, y_ref)
+    ls_f, dv_f, air_f, dist_f, gain_f, q1_f, q2_f, z0_f, y_f = map(
+        flat, (ls, dv, air, dist, gain, q1, q2, z0_ref, y_ref)
     )
     lane = lax.broadcasted_iota(jnp.int32, (8, LANES), 1)
 
@@ -276,6 +270,7 @@
                     on = table[c, pl.ds(row_of + j, 1), :] > 0.5
                     fluid = jnp.logical_and(level < 0, on)
                     air_f[c, pl.ds(base + 8 * j, 8), :] = jnp.where(fluid, 0.0, jnp.abs(level))
+                    dist_f[c, pl.ds(base + 8 * j, 8), :] = jnp.where(fluid, -level, 0.0)
             return carry
 
         return layer
@@ -287,12 +282,11 @@
                 r = base + 8 * i
                 middle = rows_at(air_f, r)
                 for c, parts in enumerate(beside(air_f, r, middle)):
-                    level = ls_f[c, pl.ds(r, 8), :]
-                    distance = -level
+                    distance = dist_f[c, pl.ds(r, 8), :]
                     most = 19.0 * distance
                     extra = added([jnp.minimum(part, most) for part in parts])
-                    fluid = jnp.logical_and(middle[c] == 0.0, level < 0)
-                    here = jnp.where(fluid, (2.0 / 3.0) * distance / (6.0 * distance + extra), 0.0)
+                    below = jnp.maximum(6.0 * distance + extra, 0.1)
+                    here = (2.0 / 3.0) * distance / below
                     gain_f[c, pl.ds(r, 8), :] = here
                     if with_q1:
                         q1_f[c, pl.ds(r, 8), :] = here * dv_f[c, pl.ds(r, 8), :]
@@ -307,10 +301,10 @@
                 q1_f[c, pl.ds(r, 8), :] = gain_f[c, pl.ds(r, 8), :] * dv_f[c, pl.ds(r, 8), :]
         return carry
 
-    def stage(source, target, own_part, sign):
+    def stage(source, target, own_part, sign, columns=range(WALK)):
         def layer(z, carry):
             base = z * PX + 4
-            for i in range(WALK):
+            for i in columns:
                 r = base + 8 * i
                 middle = rows_at(source, r)
                 for c, parts in enumerate(beside(source, r, middle)):
@@ -320,8 +314,12 @@
 
         return layer
 
-    find_z0 = stage(q1_f, z0_f, 4.0 / 3.0, 1.0)
-    find_q2 = stage(z0_f, q2_f, 2.0 / 3.0, -1.0)
+    def find_z0(columns=range(WALK)):
+        return stage(q1_f, z0_f, 4.0 / 3.0, 1.0, columns)
+
+    def find_q2(columns=range(WALK)):
+        return stage(z0_f, q2_f, 2.0 / 3.0, -1.0, columns)
+
     find_y = stage(q2_f, y_f, 4.0 / 3.0, 1.0)
 
     def finish(z, held):
@@ -333,9 +331,8 @@
             middle = rows_at(y_f, r)
             for c, parts in enumerate(beside(y_f, r, middle)):
                 here = gain_f[c, pl.ds(r, 8), :]
-                fluid = here > 0.0
-                inverse = jnp.where(fluid, 1.0 / jnp.where(fluid, here, 1.0), 0.0)
-                r0 = jnp.where(fluid, dv_f[c, pl.ds(r, 8), :], 0.0)
+                inverse = 1.0 / jnp.maximum(here, 1e-3)
+                r0 = jnp.where(here > 0.0, dv_f[c, pl.ds(r, 8), :], 0.0)
                 w0 = inverse * q2_f[c, pl.ds(r, 8), :]
                 u = inverse * ((2.0 / 3.0) * middle[c] - here * added(parts))
                 z0 = z0_f[c, pl.ds(r, 8), :]
@@ -368,39 +365,48 @@
     edges, between = (0, WALK - 1), range(1, WALK - 1)
     fill_table(4, 5)
     walk(5, 20, find_air(inner))
+    loaded(dv, 1, (0, 1))
+    send(lambda field, sx, sz, kx, kz, wave: field == "dv" and sx == 0 and wave == 1)
+    loaded(dv, 1, (2,))
+    send(lambda field, sx, sz, kx, kz, wave: field == "dv" and sx != 0 and sz == 0)
+    send(lambda field, sx, sz, kx, kz, wave: field == "dv" and sx != 0 and sz != 0)
+    send(lambda field, sx, sz, kx, kz, wave: wave == 2)
+    walk(6, 19, find_gain(between))
     for sx, sz in around:
         pl.when(exists(-sx, -sz))(lambda sx=sx, sz=sz: id_copy(sx, sz, -1).wait_recv())
     fill_table(0, 9)
     arrive_early(lambda field, sx, wave: sx == 0)
     walk(0, 4, find_air(inner))
-    walk(1, 19, find_gain(between))
+    walk(1, 5, find_gain(between))
     arrive(lambda field, sx, sz, kx, kz, wave: sz == 0 and field == "ls")
     arrive_early(lambda field, sx, wave: sx != 0 and field == "ls")
     walk(0, 20, find_air((0, 9)))
     walk(1, 19, find_gain(edges, False))
+    walk(2, 18, find_z0(range(2, 7)))
+    walk(3, 17, find_q2(range(3, 6)), group=5)
     arrive(lambda field, sx, sz, kx, kz, wave: sz == 0 and field == "dv")
     arrive_early(lambda field, sx, wave: sx != 0 and field == "dv")
     walk(1, 19, find_q1)
-    walk(2, 18, find_z0)
-    walk(3, 17, find_q2)
+    walk(2, 18, find_z0((0, 1, 7, 8)), group=4)
+    walk(3, 17, find_q2((0, 1, 2, 6, 7, 8)))
     walk(4, 16, find_y)
     held = walk(5, 15, finish, tuple(jnp.zeros((8, LANES), f32) for _ in range(6)))
 
     arrive_late(lambda field, sx, wave: wave == 1)
-    walk(21, 23, find_air(every_column))
-    walk(20, 22, find_gain(range(WALK)))
-    walk(19, 21, find_z0)
-    walk(18, 20, find_q2)
-    walk(17, 19, find_y)
-    held = walk(16, 18, finish, held)
+    walk(21, 24, find_air(every_column), group=2)
+    walk(20, 23, find_gain(range(WALK)), group=2)
+    walk(19, 22, find_z0(), group=2)
+    walk(18, 21, find_q2(), group=2)
+    walk(17, 20, find_y, group=2)
+    held = walk(16, 19, finish, held, group=2)
 
     arrive_late(lambda field, sx, wave: wave == 2)
-    walk(24, 25, find_air(every_column))
-    walk(23, 24, find_gain(range(WALK)))
-    walk(22, 23, find_z0)
-    walk(21, 22, find_q2)
-    walk(20, 21, find_y)
-    held = walk(19, 20, finish, held)
+    walk(25, 25, find_air(every_column))
+    walk(24, 24, find_gain(range(WALK)))
+    walk(23, 23, find_z0())
+    walk(22, 22, find_q2())
+    walk(21, 21, find_y)
+    held = walk(20, 20, finish, held)
 
     lane_row = lax.broadcasted_iota(jnp.int32, (1, LANES), 1)
     packed = jnp.zeros((1, LANES), f32)
@@ -487,8 +493,7 @@
         in_specs=[pl.BlockSpec(memory_space=pltpu.HBM)] * 3,
         out_specs=[pl.BlockSpec(memory_space=pltpu.VMEM)] * 6,
         scratch_shapes=[
-            pltpu.VMEM(extended, f32), pltpu.VMEM(extended, f32), pltpu.VMEM(extended, f32),
-            pltpu.VMEM(extended, f32), pltpu.VMEM(extended, f32), pltpu.VMEM(extended, f32),
+            *[pltpu.VMEM(extended, f32)] * 7,
             pltpu.VMEM((9, 1, SLOTS), jnp.int32),
             pltpu.VMEM((CH, 40, LANES), f32),
             pltpu.VMEM((8, LANES), f32),
@@ -503,7 +508,7 @@
             pltpu.SemaphoreType.DMA((2,)),
         ],
         compiler_params=pltpu.CompilerParams(
-            collective_id=0, has_side_effects=True, vmem_limit_bytes=36 * 2**20
+            collective_id=0, has_side_effects=True, vmem_limit_bytes=40 * 2**20
         ),
         name="solve",
     )(*(pltpu.with_memory_space_constraint(array, pltpu.HBM) for array in (divergence, level_set, tile_ids)))

time: 39.9 us -> 39 us (0.977)
  Pallas kernels: 39 us -> 38.1 us
    pallas_call x1, Pallas kernels: 37 us -> 36.1 us  [on_device(): pl.pallas_call(main_kernel, out_shape=[pltpu.VMEM(extended, f32)] * 2 + [...]
where the time goes in v3:
time: 39 us; the launch traced here: 38.7 us
  Pallas kernels  38.1 us (98%)
  between operations  0.64 us (2%)
    pallas_call x1, Pallas kernels, on_device(): pl.pallas_call(main_kernel, out_shape=[pltpu.VMEM(extended, f32)] * 2 + [...  36.1 us
    pallas_call x1, Pallas kernels, on_device(): pl.pallas_call(last_kernel, out_shape=[jax.ShapeDtypeStruct(divergence.sh...  2.01 us

profile of v3, /device:TPU:1, one launch (start us, length us, event | category | flops | bytes accessed | tf_op | source)
XLA Modules:
  0.0 38.7 jit_solution(14177247123347444009)
XLA Ops:
  0.6 36.1 %solve.1 = (f32[4,26,80,128]{3,2,1,0:T(8,128)S(1)}, f32[4,26,80,128]{3,2,1,0:T(8,128)S(1)}, f32[4,1024,128]{2,1,0:T(8,128)S(1)}, f32[4,1024,128]{2,1,0:T(8,128)S...) custom-call(f32[64,16,512]{2,1,0:T(8,128)} %dv_in.1, f32[64,16,512]{2,1,0:T(8,128)} %ls_in.1, s32[1,1024]{1,0:T(1,128)} %ids_in.1), custom_call_target="tpu_custom_call" | custom-call | tf_op jit(solution)/shard_map/solve/pallas_call | solution.py:490
  36.7 2.0 %update.1 = (f32[64,16,512]{2,1,0:T(8,128)}, f32[64,16,512]{2,1,0:T(8,128)}) custom-call(f32[4,26,80,128]{3,2,1,0:T(8,128)S(1)} %get-tuple-element.8.z0_ref, f32[4,26,80,128]{3,2,1,0:T(8,128)S(1)} %get-tuple-element.9.y_ref, f32[4,1024,128]{2,1,0:T(8,128)S(1)} %get-tuple-element.10.r0_ref, f32[4,1024,128]{2,1,0:T(8,128)S(1)} %get-tuple-element.11.w0_ref, ...), custom_call_target="tpu_custom_call" | custom-call | tf_op jit(solution)/shard_map/update/pallas_call | solution.py:515

commit v4 on v3

--- a/solution.py
+++ b/solution.py
@@ -15,6 +15,7 @@
 X0, Z0 = 8, 5
 PX, PZ = 80, 26
 N_GX, N_GZ = 4, 32
+DEVICES = N_GX * N_GZ
 SLOTS = 1024
 SHIFT = 1.125
 WALK = 9
@@ -53,8 +54,8 @@
 def main_kernel(
     dv_in, ls_in, ids_in,
     z0_ref, y_ref, r0_ref, w0_ref, u_ref, step_ref,
-    ls, dv, air, dist, gain, q1, q2, ids, table, sums, near_sum, far_sum,
-    load_sem, send_sem, recv_sem, id_send, id_recv, ar_send, ar_recv,
+    ls, dv, air, dist, gain, q1, q2, ids, table, sums, every_sum,
+    load_sem, send_sem, recv_sem, id_send, id_recv, ar_send, ar_recv, word_sem,
 ):
     gx, gz = lax.axis_index("gx"), lax.axis_index("gz")
     core = lax.rem(gz, 2)
@@ -87,15 +88,11 @@
     pl.when(gz == 0)(lambda: clear(0, Z0, 0, PX))
     pl.when(gz == N_GZ - 1)(lambda: clear(Z0 + NZ, 5, 0, PX))
 
-    me_near = place_z * 2 + core
-    me_far = gx * 4 + place_x
-
-    def near_peer(i):
-        return gx, place_x * 8 + (me_near ^ i)
-
-    def far_peer(i):
-        other = me_far ^ i
-        return other // 4, lax.rem(other, 4) * 8 + me_near
+    me_chip = (gx * 4 + place_x) * 4 + place_z
+
+    def sum_peer(i):
+        chip = me_chip ^ (i >> 1)
+        return chip // 16, lax.rem(chip, 16) * 2 + (core ^ (i & 1))
 
     barrier = pltpu.get_barrier_semaphore()
     around = [(sx, sz) for sx, sz in AROUND if (sx, sz) != (0, 0)]
@@ -105,10 +102,6 @@
                 barrier, inc=1, device_id=(gx + sx, gz + sz), device_id_type=MESH
             )
         )
-    for i in range(1, 8):
-        pl.semaphore_signal(barrier, inc=1, device_id=near_peer(i), device_id_type=MESH)
-    for i in range(1, 16):
-        pl.semaphore_signal(barrier, inc=1, device_id=far_peer(i), device_id_type=MESH)
     own_ids = pltpu.make_async_copy(ids_in, ids.at[4], load_sem.at[6])
     own_ids.start()
     parts = ((0, 5), (11, 5), (5, 6))
@@ -128,10 +121,39 @@
             region = array.at[:, pl.ds(Z0 + first, count), pl.ds(X0, NX)]
             pltpu.make_async_copy(region, region, load_sem.at[field * 3 + part]).wait()
 
-    peers = 22
+    peers = 0
     for sx, sz in around:
         peers = peers + exists(sx, sz).astype(jnp.int32)
     pl.semaphore_wait(barrier, peers)
+
+    reach = [(0, 1), (0, 2), (0, 4), (0, 8), (0, 16), (1, 0), (2, 0)]
+
+    def greeted(step):
+        dx, dz = reach[step]
+        for sign in (-1, 1):
+            if dx:
+                ok = gx + dx < N_GX if sign > 0 else gx >= dx
+            else:
+                ok = gz + dz < N_GZ if sign > 0 else gz >= dz
+            yield ok, (gx + sign * dx, gz + sign * dz)
+
+    def greet(step):
+        for ok, peer in greeted(step):
+            pl.when(ok)(
+                lambda peer=peer: pl.semaphore_signal(
+                    word_sem.at[step], inc=1, device_id=peer, device_id_type=MESH
+                )
+            )
+
+    def heed(step):
+        count = 0
+        for ok, _ in greeted(step):
+            count = count + ok.astype(jnp.int32)
+        pl.semaphore_wait(word_sem.at[step], count)
+        if step + 1 < len(reach):
+            greet(step + 1)
+
+    greet(0)
 
     def id_copy(sx, sz, peer=1):
         target = (1 - sx) * 3 + (1 - sz)
@@ -371,27 +393,34 @@
     send(lambda field, sx, sz, kx, kz, wave: field == "dv" and sx != 0 and sz == 0)
     send(lambda field, sx, sz, kx, kz, wave: field == "dv" and sx != 0 and sz != 0)
     send(lambda field, sx, sz, kx, kz, wave: wave == 2)
+    heed(0)
     walk(6, 19, find_gain(between))
+    heed(1)
     for sx, sz in around:
         pl.when(exists(-sx, -sz))(lambda sx=sx, sz=sz: id_copy(sx, sz, -1).wait_recv())
     fill_table(0, 9)
     arrive_early(lambda field, sx, wave: sx == 0)
     walk(0, 4, find_air(inner))
     walk(1, 5, find_gain(between))
+    heed(2)
     arrive(lambda field, sx, sz, kx, kz, wave: sz == 0 and field == "ls")
     arrive_early(lambda field, sx, wave: sx != 0 and field == "ls")
     walk(0, 20, find_air((0, 9)))
     walk(1, 19, find_gain(edges, False))
+    heed(3)
     walk(2, 18, find_z0(range(2, 7)))
     walk(3, 17, find_q2(range(3, 6)), group=5)
     arrive(lambda field, sx, sz, kx, kz, wave: sz == 0 and field == "dv")
     arrive_early(lambda field, sx, wave: sx != 0 and field == "dv")
+    heed(4)
     walk(1, 19, find_q1)
     walk(2, 18, find_z0((0, 1, 7, 8)), group=4)
     walk(3, 17, find_q2((0, 1, 2, 6, 7, 8)))
+    heed(5)
     walk(4, 16, find_y)
     held = walk(5, 15, finish, tuple(jnp.zeros((8, LANES), f32) for _ in range(6)))
 
+    heed(6)
     arrive_late(lambda field, sx, wave: wave == 1)
     walk(21, 24, find_air(every_column), group=2)
     walk(20, 23, find_gain(range(WALK)), group=2)
@@ -414,24 +443,21 @@
         whole = jnp.sum(jnp.sum(total, axis=0, keepdims=True), axis=1, keepdims=True)
         packed = jnp.where(lane_row == k, whole, packed)
 
-    def all_sum(value, buffer, count, peer, number):
-        buffer[pl.ds(0, 1), :] = value
-        for i in range(1, count):
-            pltpu.make_async_remote_copy(
-                buffer.at[pl.ds(0, 1)], buffer.at[pl.ds(i, 1)], ar_send.at[number], ar_recv.at[number],
-                device_id=peer(i), device_id_type=MESH,
-            ).start()
-        every = pltpu.make_async_remote_copy(
-            buffer.at[pl.ds(0, count - 1)], buffer.at[pl.ds(1, count - 1)], ar_send.at[number], ar_recv.at[number],
-            device_id=peer(1), device_id_type=MESH,
-        )
-        every.wait_recv()
-        result = jnp.sum(buffer[...], axis=0, keepdims=True)
-        return result, every
-
-    part, sent_near = all_sum(packed, near_sum, 8, near_peer, 0)
-    whole, sent_far = all_sum(part, far_sum, 16, far_peer, 1)
-    sums[pl.ds(0, 1), :] = whole
+    def ring_distance(i):
+        return sum((0, 1, 2, 1)[(i >> shift) & 3] for shift in (1, 3, 5))
+
+    every_sum[pl.ds(0, 1), :] = packed
+    for i in sorted(range(1, DEVICES), key=lambda i: -ring_distance(i)):
+        pltpu.make_async_remote_copy(
+            every_sum.at[pl.ds(0, 1)], every_sum.at[pl.ds(i, 1)], ar_send.at[0], ar_recv.at[0],
+            device_id=sum_peer(i), device_id_type=MESH,
+        ).start()
+    sent = pltpu.make_async_remote_copy(
+        every_sum.at[pl.ds(0, DEVICES - 1)], every_sum.at[pl.ds(1, DEVICES - 1)], ar_send.at[0], ar_recv.at[0],
+        device_id=sum_peer(1), device_id_type=MESH,
+    )
+    sent.wait_recv()
+    sums[pl.ds(0, 1), :] = jnp.sum(every_sum[...], axis=0, keepdims=True)
     gamma0, delta0, eta, theta, gamma_s, delta_s = (sums[pl.ds(0, 1), pl.ds(k, 1)] for k in range(6))
     alpha0 = gamma0 / delta0
     off = alpha0 - SHIFT
@@ -449,8 +475,7 @@
         pl.when(exists(sx, sz))(lambda number=number: layer_copy(number).wait_send())
     for sx, sz in around:
         pl.when(exists(sx, sz))(lambda sx=sx, sz=sz: id_copy(sx, sz).wait_send())
-    sent_near.wait_send()
-    sent_far.wait_send()
+    sent.wait_send()
 
 
 def last_kernel(z0_ref, y_ref, r0_ref, w0_ref, u_ref, step_ref, p_out, r_out, p_buf, r_buf, sem):
@@ -497,15 +522,15 @@
             pltpu.VMEM((9, 1, SLOTS), jnp.int32),
             pltpu.VMEM((CH, 40, LANES), f32),
             pltpu.VMEM((8, LANES), f32),
-            pltpu.VMEM((8, LANES), f32),
-            pltpu.VMEM((16, LANES), f32),
+            pltpu.VMEM((DEVICES, LANES), f32),
             pltpu.SemaphoreType.DMA((7,)),
             pltpu.SemaphoreType.DMA((len(MESSAGES),)),
             pltpu.SemaphoreType.DMA((len(MESSAGES),)),
             pltpu.SemaphoreType.DMA((9,)),
             pltpu.SemaphoreType.DMA((9,)),
-            pltpu.SemaphoreType.DMA((2,)),
-            pltpu.SemaphoreType.DMA((2,)),
+            pltpu.SemaphoreType.DMA((1,)),
+            pltpu.SemaphoreType.DMA((1,)),
+            pltpu.SemaphoreType.REGULAR((7,)),
         ],
         compiler_params=pltpu.CompilerParams(
             collective_id=0, has_side_effects=True, vmem_limit_bytes=40 * 2**20

time: 39 us -> 37.3 us (0.956)
  Pallas kernels: 38.1 us -> 36.5 us
    pallas_call x1, Pallas kernels: 36.1 us -> 34.5 us  [on_device(): pl.pallas_call(main_kernel, out_shape=[pltpu.VMEM(extended, f32)] * 2 + [...]
where the time goes in v4:
time: 37.3 us; the launch traced here: 37.2 us
  Pallas kernels  36.5 us (98%)
  between operations  0.64 us (2%)
    pallas_call x1, Pallas kernels, on_device(): pl.pallas_call(main_kernel, out_shape=[pltpu.VMEM(extended, f32)] * 2 + [...  34.5 us
    pallas_call x1, Pallas kernels, on_device(): pl.pallas_call(last_kernel, out_shape=[jax.ShapeDtypeStruct(divergence.sh...  2.01 us

profile of v4, /device:TPU:1, one launch (start us, length us, event | category | flops | bytes accessed | tf_op | source)
XLA Modules:
  0.0 37.2 jit_solution(9290494291612907055)
XLA Ops:
  0.6 34.5 %solve.1 = (f32[4,26,80,128]{3,2,1,0:T(8,128)S(1)}, f32[4,26,80,128]{3,2,1,0:T(8,128)S(1)}, f32[4,1024,128]{2,1,0:T(8,128)S(1)}, f32[4,1024,128]{2,1,0:T(8,128)S...) custom-call(f32[64,16,512]{2,1,0:T(8,128)} %dv_in.1, f32[64,16,512]{2,1,0:T(8,128)} %ls_in.1, s32[1,1024]{1,0:T(1,128)} %ids_in.1), custom_call_target="tpu_custom_call" | custom-call | tf_op jit(solution)/shard_map/solve/pallas_call | solution.py:515
  35.1 2.0 %update.1 = (f32[64,16,512]{2,1,0:T(8,128)}, f32[64,16,512]{2,1,0:T(8,128)}) custom-call(f32[4,26,80,128]{3,2,1,0:T(8,128)S(1)} %get-tuple-element.8.z0_ref, f32[4,26,80,128]{3,2,1,0:T(8,128)S(1)} %get-tuple-element.9.y_ref, f32[4,1024,128]{2,1,0:T(8,128)S(1)} %get-tuple-element.10.r0_ref, f32[4,1024,128]{2,1,0:T(8,128)S(1)} %get-tuple-element.11.w0_ref, ...), custom_call_target="tpu_custom_call" | custom-call | tf_op jit(solution)/shard_map/update/pallas_call | solution.py:540

commit v5 on v4

--- a/solution.py
+++ b/solution.py
@@ -362,8 +362,8 @@
                 r0_ref[c, pl.ds(out + 8 * i, 8), :] = r0
                 w0_ref[c, pl.ds(out + 8 * i, 8), :] = w0
                 u_ref[c, pl.ds(out + 8 * i, 8), :] = u
-                r_s, z_s, w_s = r0 - SHIFT * w0, z0 - SHIFT * y, w0 - SHIFT * u
-                products = (r0 * z0, w0 * z0, w0 * y, u * y, r_s * z_s, w_s * z_s)
+                z_s = z0 - SHIFT * y
+                products = (r0 * z0, w0 * z0, r0 * z_s, w0 * z_s, u * z_s)
                 held = [total + term for total, term in zip(held, products)]
         return tuple(held)
 
@@ -408,25 +408,25 @@
     walk(0, 20, find_air((0, 9)))
     walk(1, 19, find_gain(edges, False))
     heed(3)
-    walk(2, 18, find_z0(range(2, 7)))
+    walk(2, 18, find_z0(range(2, 7)), group=6)
     walk(3, 17, find_q2(range(3, 6)), group=5)
     arrive(lambda field, sx, sz, kx, kz, wave: sz == 0 and field == "dv")
     arrive_early(lambda field, sx, wave: sx != 0 and field == "dv")
     heed(4)
     walk(1, 19, find_q1)
-    walk(2, 18, find_z0((0, 1, 7, 8)), group=4)
-    walk(3, 17, find_q2((0, 1, 2, 6, 7, 8)))
+    walk(2, 18, find_z0((0, 1, 7, 8)), group=6)
+    walk(3, 17, find_q2((0, 1, 2, 6, 7, 8)), group=5)
     heed(5)
-    walk(4, 16, find_y)
-    held = walk(5, 15, finish, tuple(jnp.zeros((8, LANES), f32) for _ in range(6)))
+    walk(4, 16, find_y, group=5)
+    held = walk(5, 15, finish, tuple(jnp.zeros((8, LANES), f32) for _ in range(5)), group=3)
 
     heed(6)
     arrive_late(lambda field, sx, wave: wave == 1)
     walk(21, 24, find_air(every_column), group=2)
     walk(20, 23, find_gain(range(WALK)), group=2)
-    walk(19, 22, find_z0(), group=2)
-    walk(18, 21, find_q2(), group=2)
-    walk(17, 20, find_y, group=2)
+    walk(19, 22, find_z0(), group=4)
+    walk(18, 21, find_q2(), group=4)
+    walk(17, 20, find_y, group=4)
     held = walk(16, 19, finish, held, group=2)
 
     arrive_late(lambda field, sx, wave: wave == 2)
@@ -458,10 +458,12 @@
     )
     sent.wait_recv()
     sums[pl.ds(0, 1), :] = jnp.sum(every_sum[...], axis=0, keepdims=True)
-    gamma0, delta0, eta, theta, gamma_s, delta_s = (sums[pl.ds(0, 1), pl.ds(k, 1)] for k in range(6))
+    gamma0, delta0, first, kappa, lam = (sums[pl.ds(0, 1), pl.ds(k, 1)] for k in range(5))
+    eta = (delta0 - kappa) / SHIFT
+    theta = (eta - lam) / SHIFT
+    gamma_s, delta_s = first - SHIFT * kappa, kappa - SHIFT * lam
     alpha0 = gamma0 / delta0
     off = alpha0 - SHIFT
-    kappa, lam = delta0 - SHIFT * eta, eta - SHIFT * theta
     gamma1 = gamma_s - 2.0 * off * kappa + off * off * eta
     delta1 = delta_s - 2.0 * off * lam + off * off * theta
     beta = gamma1 / gamma0

time: 37.3 us -> 36 us (0.965)
  Pallas kernels: 36.5 us -> 35.2 us
    pallas_call x1, Pallas kernels: 34.5 us -> 33.2 us  [on_device(): pl.pallas_call(main_kernel, out_shape=[pltpu.VMEM(extended, f32)] * 2 + [...]
where the time goes in v5:
time: 36 us; the launch traced here: 35.9 us
  Pallas kernels  35.2 us (98%)
  between operations  0.64 us (2%)
    pallas_call x1, Pallas kernels, on_device(): pl.pallas_call(main_kernel, out_shape=[pltpu.VMEM(extended, f32)] * 2 + [...  33.2 us
    pallas_call x1, Pallas kernels, on_device(): pl.pallas_call(last_kernel, out_shape=[jax.ShapeDtypeStruct(divergence.sh...  2.01 us

profile of v5, /device:TPU:1, one launch (start us, length us, event | category | flops | bytes accessed | tf_op | source)
XLA Modules:
  0.0 35.9 jit_solution(29551709315434530)
XLA Ops:
  0.6 33.2 %solve.1 = (f32[4,26,80,128]{3,2,1,0:T(8,128)S(1)}, f32[4,26,80,128]{3,2,1,0:T(8,128)S(1)}, f32[4,1024,128]{2,1,0:T(8,128)S(1)}, f32[4,1024,128]{2,1,0:T(8,128)S...) custom-call(f32[64,16,512]{2,1,0:T(8,128)} %dv_in.1, f32[64,16,512]{2,1,0:T(8,128)} %ls_in.1, s32[1,1024]{1,0:T(1,128)} %ids_in.1), custom_call_target="tpu_custom_call" | custom-call | tf_op jit(solution)/shard_map/solve/pallas_call | solution.py:517
  33.9 2.0 %update.1 = (f32[64,16,512]{2,1,0:T(8,128)}, f32[64,16,512]{2,1,0:T(8,128)}) custom-call(f32[4,26,80,128]{3,2,1,0:T(8,128)S(1)} %get-tuple-element.8.z0_ref, f32[4,26,80,128]{3,2,1,0:T(8,128)S(1)} %get-tuple-element.9.y_ref, f32[4,1024,128]{2,1,0:T(8,128)S(1)} %get-tuple-element.10.r0_ref, f32[4,1024,128]{2,1,0:T(8,128)S(1)} %get-tuple-element.11.w0_ref, ...), custom_call_target="tpu_custom_call" | custom-call | tf_op jit(solution)/shard_map/update/pallas_call | solution.py:542

commit v6 on v5

--- a/solution.py
+++ b/solution.py
@@ -189,11 +189,6 @@
     own_ids.wait()
     for sx, sz in around:
         pl.when(exists(sx, sz))(lambda sx=sx, sz=sz: id_copy(sx, sz).start())
-    loaded(ls, 0, (0, 1))
-    send(lambda field, sx, sz, kx, kz, wave: field == "ls" and sx == 0 and wave == 1)
-    loaded(ls, 0, (2,))
-    send(lambda field, sx, sz, kx, kz, wave: field == "ls" and sx != 0 and sz == 0)
-    send(lambda field, sx, sz, kx, kz, wave: field == "ls" and sx != 0 and sz != 0)
 
     row = lax.broadcasted_iota(jnp.int32, (40, 1), 0)
     row_z = (row >= 10).astype(jnp.int32) + (row >= 20).astype(jnp.int32) + (row >= 30).astype(jnp.int32)
@@ -386,6 +381,11 @@
     every_column, inner = range(10), range(1, 9)
     edges, between = (0, WALK - 1), range(1, WALK - 1)
     fill_table(4, 5)
+    loaded(ls, 0, (0, 1))
+    send(lambda field, sx, sz, kx, kz, wave: field == "ls" and sx == 0 and wave == 1)
+    loaded(ls, 0, (2,))
+    send(lambda field, sx, sz, kx, kz, wave: field == "ls" and sx != 0 and sz == 0)
+    send(lambda field, sx, sz, kx, kz, wave: field == "ls" and sx != 0 and sz != 0)
     walk(5, 20, find_air(inner))
     loaded(dv, 1, (0, 1))
     send(lambda field, sx, sz, kx, kz, wave: field == "dv" and sx == 0 and wave == 1)

time: 36 us -> 36 us (level)
  no operation moved by 1% of the time
where the time goes in v6:
time: 36 us; the launch traced here: 35.9 us
  Pallas kernels  35.3 us (98%)
  between operations  0.64 us (2%)
    pallas_call x1, Pallas kernels, on_device(): pl.pallas_call(main_kernel, out_shape=[pltpu.VMEM(extended, f32)] * 2 + [...  33.3 us
    pallas_call x1, Pallas kernels, on_device(): pl.pallas_call(last_kernel, out_shape=[jax.ShapeDtypeStruct(divergence.sh...  2.01 us

profile of v6, /device:TPU:1, one launch (start us, length us, event | category | flops | bytes accessed | tf_op | source)
XLA Modules:
  0.0 35.9 jit_solution(16035073900064114463)
XLA Ops:
  0.6 33.3 %solve.1 = (f32[4,26,80,128]{3,2,1,0:T(8,128)S(1)}, f32[4,26,80,128]{3,2,1,0:T(8,128)S(1)}, f32[4,1024,128]{2,1,0:T(8,128)S(1)}, f32[4,1024,128]{2,1,0:T(8,128)S...) custom-call(f32[64,16,512]{2,1,0:T(8,128)} %dv_in.1, f32[64,16,512]{2,1,0:T(8,128)} %ls_in.1, s32[1,1024]{1,0:T(1,128)} %ids_in.1), custom_call_target="tpu_custom_call" | custom-call | tf_op jit(solution)/shard_map/solve/pallas_call | solution.py:517
  33.9 2.0 %update.1 = (f32[64,16,512]{2,1,0:T(8,128)}, f32[64,16,512]{2,1,0:T(8,128)}) custom-call(f32[4,26,80,128]{3,2,1,0:T(8,128)S(1)} %get-tuple-element.8.z0_ref, f32[4,26,80,128]{3,2,1,0:T(8,128)S(1)} %get-tuple-element.9.y_ref, f32[4,1024,128]{2,1,0:T(8,128)S(1)} %get-tuple-element.10.r0_ref, f32[4,1024,128]{2,1,0:T(8,128)S(1)} %get-tuple-element.11.w0_ref, ...), custom_call_target="tpu_custom_call" | custom-call | tf_op jit(solution)/shard_map/update/pallas_call | solution.py:542
